TPU v7x, 256 devices: a whole 4x4x8 slice. The times are simulated.
256 devices in a mesh: grp: 16 (over x, y), dev: 16 (over z, core).
Axes of the slice: x: 4, y: 4, z: 8, core: 2. Of those that a mesh axis runs over, the one named last changes fastest.
Arguments:
- acts: bfloat16 [65536, 12288], P(('grp', 'dev')), may hold values from -6 to 6
- grads_out: bfloat16 [65536, 64], P(('grp', 'dev')), may hold values from -0.375 to 0.375
- residual_in: float32 [256, 64, 12288], P(('grp', 'dev')), may hold values from -6 to 6
- sel_index: int32 [256, 64], P(('grp', 'dev')), may hold values from 0 to 6143, as said below
- sel_count: int32 [256], P(('grp', 'dev')), may hold values from 16 to 64, as said below
- momentum_in: float32 [64, 12288], P(None, 'dev'), may hold values from -6 to 6
Outputs:
- residual_out: float32 [256, 64, 12288], P(('grp', 'dev'))
- momentum_out: float32 [64, 12288], P(None, 'dev')
Inputs may be any that keep to these rules, and one draw needn't show every extreme that they name: `sel_index`: the 64 numbers of a row are distinct. `sel_count`: equal to 64 on some device in every draw.
All inputs are finite; a program needn't handle non-finite values.
Results may differ from a plain program's by a relative error of at most 0.0003.
Values sent between devices are 32-bit elements; how exact they have to be, the bound alone decides.
No kernel may reach another device: no remote copies, remote signals or barrier semaphores. Data moves between devices by JAX's collectives and lax.ppermute only.
A program may use at most 64 MiB of HBM per device.

v0:
```python
import jax
import jax.numpy as jnp
from jax import lax
from jax.sharding import PartitionSpec as P

momentum_decay = 0.9


def side_by_side(arrays, axis, dim, along):
    columns = [a.reshape(*a.shape[:along], -1) for a in arrays]
    both = jnp.concatenate(columns, axis=along)
    filled, at, done = (lax.all_gather(both, axis, axis=dim, tiled=True), 0, [])
    for a, column in zip(arrays, columns):
        share = filled[..., at : at + column.shape[along]]
        done.append(share.reshape(*share.shape[:along], *a.shape[along:]))
        at += column.shape[along]
    return tuple(done)


def rows_for(lines, count):
    spare = -lines.shape[0] % count
    if not spare:
        return lines
    return jnp.concatenate([lines, jnp.zeros((spare, *lines.shape[1:]), lines.dtype)])


def laid_out(blocks, dim):
    lengths = list(blocks.shape[1:])
    lengths[dim] *= blocks.shape[0]
    return jnp.moveaxis(blocks, 0, dim).reshape(lengths)


def copy_for_each(shard, axis):
    count = lax.axis_size(axis)
    return lax.all_to_all(
        jnp.broadcast_to(shard[None], (count, *shard.shape)), axis, 0, 0, tiled=True
    )


def gathered_copies(shard, axis, dim):
    return laid_out(copy_for_each(shard, axis), dim)


def cut_along(shard, dim, count):
    before, after = (shard.shape[:dim], shard.shape[dim + 1 :])
    return jnp.moveaxis(shard.reshape(*before, count, -1, *after), dim, 0)


def sent_and_summed(shard, axis, dim):
    count = lax.axis_size(axis)
    blocks = lax.all_to_all(cut_along(shard, dim, count), axis, 0, 0, tiled=True)
    return jnp.sum(blocks, axis=0)


def sum_by_parts(shard, axes):
    lines = shard.reshape(-1, shard.shape[-1])
    padded = rows_for(lines, lax.axis_size(axes))
    whole = gathered_copies(sent_and_summed(padded, axes, 0), axes, 0)
    return lax.slice_in_dim(whole, 0, len(lines)).reshape(shard.shape)


def local(acts, grads_out, residual_in, sel_index, sel_count, momentum_in):
    width = acts.shape[1]
    columns = grads_out.shape[1]
    slots = sel_index.shape[1]
    n_blocks = columns * width // 128
    part_width = momentum_in.shape[1]
    local_grad = lax.dot_general(
        grads_out, acts, (((0,), (0,)), ((), ())), preferred_element_type=jnp.float32
    )
    summed = residual_in[0] + local_grad
    blocks = summed.reshape(n_blocks, 128)
    chosen = sel_index[0]
    valid_rows = (jnp.arange(slots, dtype=jnp.int32) < sel_count[0]).astype(jnp.float32)
    picked = blocks[chosen] * valid_rows[:, None]
    marked = jnp.zeros((n_blocks,), jnp.float32).at[chosen].max(valid_rows)
    kept = (blocks * (1.0 - marked)[:, None]).reshape(1, columns, width)
    labels = chosen.astype(jnp.float32)
    group_vals, group_labels = side_by_side((picked, labels), "dev", 0, 1)
    numbers = group_labels.astype(jnp.int32)
    row_blocks = width // 128
    own_blocks = part_width // 128
    block_row = numbers // row_blocks
    block_col = numbers % row_blocks
    owner = block_col // own_blocks
    owned = (owner == lax.axis_index("dev")).astype(jnp.float32)
    local_index = block_row * own_blocks + block_col % own_blocks
    partial_sum = jnp.zeros((columns * own_blocks, 128), jnp.float32)
    partial_sum = partial_sum.at[local_index].add(group_vals * owned[:, None])
    total = sum_by_parts(partial_sum.reshape(columns, part_width), "grp")
    momentum_out = momentum_decay * momentum_in + total
    return (kept, momentum_out)


def solution(mesh):
    placed = (
        P(("grp", "dev"), None),
        P(("grp", "dev"), None),
        P(("grp", "dev"), None, None),
        P(("grp", "dev"), None),
        P(("grp", "dev")),
        P(None, "dev"),
    )
    return jax.shard_map(
        local,
        mesh=mesh,
        in_specs=placed,
        out_specs=(P(("grp", "dev"), None, None), P(None, "dev")),
        check_vma=False,
    )
```

profile of v0, /device:TPU:1, one launch (start us, length us, event | category | flops | bytes accessed | tf_op | source)
XLA Modules:
  0.0 76.3 jit_solution(15910995040014286254)
XLA Ops:
  0.6 0.0 copy-start
  0.6 0.7 fusion.14
  1.3 0.7 bitcast_convert_fusion
  2.0 0.0 copy-done
  2.0 4.9 %convolution_add_fusion = f32[64,12288]{1,0:T(8,128)S(1)} fusion(bf16[256,64]{0,1:T(8,128)(2,1)S(1)} %copy-done, bf16[256,12288]{1,0:T(8,128)(2,1)} %param.6, f32[1,64,12288]{2,1,0:T(8,128)} %param.8), kind=kOutput, calls=%fused_computation.3 | convolution fusion | flops 403439616 | bytes 12615680 | tf_op jit(solution)/shard_map/dot_general | solution.py:68
  6.9 1.9 %reshape.67 = f32[6144,128]{1,0:T(8,128)} reshape(f32[64,12288]{1,0:T(8,128)S(1)} %convolution_add_fusion) | data formatting | bytes 6291456 | tf_op jit(solution)/shard_map/reshape | solution.py:72
  9.5 0.1 copy.13
  9.6 2.5 %gather_fusion = f32[64,128]{1,0:T(8,128)S(1)} fusion(f32[6144,128]{1,0:T(8,128)} %reshape.67, s32[1024]{0:T(1024)S(1)} %pad_clamp_fusion), kind=kCustom, calls=%fused_computation | custom fusion | bytes 65792 | tf_op jit(solution)/shard_map/gather | solution.py:75
  12.1 0.1 broadcast_multiply_fusion
  12.1 25.6 %all_gather.3 = f32[1024,129]{1,0:T(8,128)} all-gather(f32[64,129]{1,0:T(8,128)S(1)} %pad_maximum_fusion), channel_id=1, replica_groups=mesh['grp'=16,'dev'=16] {'dev'}, dimensions={0}, use_global_device_ids=true | all-gather | bytes 561408 | tf_op jit(solution)/shard_map/all_gather | solution.py:12
  37.7 1.9 %convert_reduce_fusion = (f32[1024]{0:T(1024)S(1)}, pred[1024,1]{1,0:T(8,128)(4,1)S(1)}) fusion(f32[1024,129]{1,0:T(8,128)} %all_gather.3, s32[]{:T(128)S(6)} %axis_index.12), kind=kLoop, calls=%fused_computation.17 | loop fusion | flops 17408 | bytes 9220 | tf_op jit(solution)/shard_map/mul | solution.py:89
  39.6 2.0 %fusion.5 = s32[1024]{0:T(1024)S(1)} fusion(pred[1024,1]{1,0:T(8,128)(4,1)S(1)} %get-tuple-element.3, f32[1024,129]{1,0:T(8,128)} %all_gather.3), kind=kLoop, calls=%fused_computation.20 | loop fusion | flops 23552 | bytes 9216 | tf_op jit(solution)/shard_map/select_n | solution.py:89
  41.6 7.0 %scatter_custom_fusion.1 = f32[384,128]{1,0:T(8,128)S(1)} fusion(s32[1024]{0:T(1024)S(1)} %fusion.5, f32[1024,129]{1,0:T(8,128)} %all_gather.3, f32[1024]{0:T(1024)S(1)} %get-tuple-element.2, f32[]{:T(128)} %constant.41.clone.1), kind=kCustom, calls=%fused_computation.15 | custom fusion | flops 262144 | bytes 725504 | tf_op jit(solution)/shard_map/scatter-add | solution.py:89
  48.6 0.8 reshape_reshape.3
  49.4 6.8 %all-to-all-start = ((f32[16,4,768]{2,1,0:T(4,128)}), f32[16,4,768]{2,1,0:T(4,128)S(1)}, u32[]{:S(2)}, u32[]{:S(2)}) async-start(f32[16,4,768]{2,1,0:T(4,128)} %reshape_reshape.3), calls=%async_computation | async-start | bytes 393216 | tf_op jit(solution)/shard_map/all_to_all | solution.py:51
  56.1 0.9 %scatter_custom_fusion = f32[6144]{0:T(1024)S(1)} fusion(s32[64]{0:T(128)S(1)} %fusion.14, f32[64]{0:T(128)S(1)} %compare_convert_fusion, f32[]{:T(128)} %constant.41.clone.1), kind=kCustom, calls=%fused_computation.31 | custom fusion | flops 64 | bytes 24580 | tf_op jit(solution)/shard_map/scatter-max | solution.py:76
  57.1 0.1 mul.50
  57.2 6.0 %all-to-all-done = f32[16,4,768]{2,1,0:T(4,128)S(1)} async-done(((f32[16,4,768]{2,1,0:T(4,128)}), f32[16,4,768]{2,1,0:T(4,128)S(1)}, u32[]{:S(2)}, u32[]{:S(2)}) %all-to-all-start) | async-done | bytes 196640 | tf_op jit(solution)/shard_map/all_to_all | solution.py:51
  63.2 0.7 broadcast_in_dim.8
  63.9 3.8 %all-to-all-start.1 = ((f32[16,4,768]{2,1,0:T(4,128)}), f32[16,4,768]{2,1,0:T(4,128)S(1)}, u32[]{:S(2)}, u32[]{:S(2)}) async-start(f32[16,4,768]{2,1,0:T(4,128)} %broadcast_in_dim.8), calls=%async_computation.1 | async-start | bytes 393216 | tf_op jit(solution)/shard_map/all_to_all | solution.py:35
  67.7 0.9 %mul.51 = f32[64,96,128]{2,1,0:T(8,128)S(1)} broadcast(f32[64,96]{1,0:T(8,128)S(1)} %mul.50), dimensions={0,1} | broadcast | bytes 3170304 | tf_op jit(solution)/shard_map/mul | solution.py:77
  68.6 3.6 %fusion = f32[1,64,12288]{2,1,0:T(8,128)} fusion(f32[64,12288]{1,0:T(8,128)S(1)} %convolution_add_fusion, f32[8,8,96,128]{3,2,1,0:T(8,128)S(1)} %bitcast.18), kind=kLoop, calls=%fused_computation.5 | loop fusion | flops 786432 | bytes 9437184 | tf_op jit(solution)/shard_map/mul | solution.py:77
  72.2 2.4 %all-to-all-done.1 = f32[16,4,768]{2,1,0:T(4,128)S(1)} async-done(((f32[16,4,768]{2,1,0:T(4,128)}), f32[16,4,768]{2,1,0:T(4,128)S(1)}, u32[]{:S(2)}, u32[]{:S(2)}) %all-to-all-start.1) | async-done | bytes 196640 | tf_op jit(solution)/shard_map/all_to_all | solution.py:35
  74.6 0.1 reshape.68
  74.7 1.6 %multiply_add_fusion = f32[64,768]{1,0:T(8,128)} fusion(f32[64,768]{1,0:T(8,128)S(1)} %reshape.68, f32[64,768]{1,0:T(8,128)} %param.11), kind=kLoop, calls=%fused_computation.27 | loop fusion | flops 98304 | bytes 589824 | tf_op jit(solution)/shard_map/add | solution.py:91
  (5 shorter events, 0.1 us)
Async XLA Ops:
  0.6 1.3 %copy-start = (bf16[256,64]{0,1:T(8,128)(2,1)S(1)}, bf16[256,64]{0,1:T(8,128)(2,1)}, u32[]{:S(2)}) copy-start(bf16[256,64]{0,1:T(8,128)(2,1)} %param.7) | copy-start | bytes 98308
  49.4 13.8 %all-to-all-start = ((f32[16,4,768]{2,1,0:T(4,128)}), f32[16,4,768]{2,1,0:T(4,128)S(1)}, u32[]{:S(2)}, u32[]{:S(2)}) async-start(f32[16,4,768]{2,1,0:T(4,128)} %reshape_reshape.3), calls=%async_computation | async-start | bytes 393216 | tf_op jit(solution)/shard_map/all_to_all | solution.py:51
  63.9 10.7 %all-to-all-start.1 = ((f32[16,4,768]{2,1,0:T(4,128)}), f32[16,4,768]{2,1,0:T(4,128)S(1)}, u32[]{:S(2)}, u32[]{:S(2)}) async-start(f32[16,4,768]{2,1,0:T(4,128)} %broadcast_in_dim.8), calls=%async_computation.1 | async-start | bytes 393216 | tf_op jit(solution)/shard_map/all_to_all | solution.py:35
where the time goes:
time: 77 us; the launch traced here: 76.3 us
  blocking collectives  25.6 us (33%)
  other arithmetic  18.6 us (24%)
  starting transfers between devices  10.6 us (14%)
  waiting for transfers between devices  8.39 us (11%)
  local copies, waits for them, and re-layouts  6.97 us (9%)
  matrix products  4.91 us (6%)
  between operations  1.36 us (2%)
    all_gather x1, blocking collectives, side_by_side(): filled, at, done = (lax.all_gather(both, axis, axis=dim, tiled=True), 0, [])  25.6 us
    scatter-add x1, other arithmetic, local(): partial_sum = partial_sum.at[local_index].add(group_vals * owned[:, None])  7 us
    all_to_all x1, starting transfers between devices, sent_and_summed(): lax.all_to_all(cut_along(shard, dim, count), axis, 0, 0, tiled=True)  6.75 us
    all_to_all x1, waiting for transfers between devices, sent_and_summed(): lax.all_to_all(cut_along(shard, dim, count), axis, 0, 0, tiled=True)  5.98 us
    dot_general x1, matrix products, local(): lax.dot_general(grads_out, acts, (((0,), (0,)), ((), ())), preferred_elem...  4.91 us
    all_to_all x1, starting transfers between devices, copy_for_each(): lax.all_to_all(jnp.broadcast_to(shard[None], (count, *shard.shape)), axis...  3.81 us
    mul x1, other arithmetic, local(): kept = (blocks * (1.0 - marked)[:, None]).reshape(1, columns, width)  3.64 us
    gather x1, local copies, waits for them, and re-layouts, local(): picked = blocks[chosen] * valid_rows[:, None]  2.48 us
  transfers between devices with their start and end apart: 2, of which 2 were waited for; matrix products, arithmetic and copies ran while one was open for 7% of the time, Pallas kernels for 0%

commit v1 on v0

v1 whole, which is shorter than its diff:
```python
import jax
import jax.numpy as jnp
from jax import lax
from jax.experimental import pallas as pl
from jax.experimental.pallas import tpu as pltpu
from jax.sharding import PartitionSpec as P

momentum_decay = 0.9
lanes = 128
sublanes = 8
chunk_count = 8


def pick_kernel(index_s, count_s, index_v, grads_t, acts, residual, grad_ref, out_ref,
                acts_v, tiles, codes_v, acts_sems, tile_sem, *, row_blocks, own_blocks):
    row_tiles = grad_ref.shape[0]
    slots = index_s.shape[1]
    chunk = row_blocks * lanes // chunk_count
    chunk_blocks = row_blocks // chunk_count
    members = out_ref.shape[0]
    half = own_blocks // 2
    part = half * sublanes

    def acts_copy(i):
        at = pl.ds(pl.multiple_of(i * chunk, lanes), chunk)
        return pltpu.make_async_copy(acts.at[:, at], acts_v.at[i], acts_sems.at[i])

    for i in range(chunk_count):
        acts_copy(i).start()

    def fetch(s, carry):
        block = index_s[0, s]
        row = block // row_blocks
        col = block - row * row_blocks
        pltpu.make_async_copy(residual.at[row // sublanes, col], tiles.at[s], tile_sem).start()
        return carry

    lax.fori_loop(0, slots, fetch, 0, unroll=8)

    count = count_s[0]
    block = index_v[...]
    row = (block * 43691) >> 22
    col = block - row * row_blocks
    owner = (col * 10923) >> 16
    inner = col - owner * own_blocks
    side = jnp.where(inner >= half, 1, 0)
    share = (row >> 3) * 2 + side
    target = owner * part + (inner - side * half) * sublanes + (row & 7)
    code = share * (part * row_blocks // own_blocks) + target
    slot = lax.broadcasted_iota(jnp.int32, code.shape, 1)
    code = jnp.where(slot < count, code, -1).astype(jnp.float32)
    codes_v[...] = jnp.zeros_like(codes_v)
    codes_v[0:1, 0:slots] = code
    both = codes_v[...]
    both = both + pltpu.roll(both, slots, 1)
    out_ref[0, slots:slots + sublanes, :] = both

    def multiply(i, carry):
        acts_copy(i).wait()
        grad = jnp.dot(grads_t[...], acts_v[i], preferred_element_type=jnp.float32)
        for r in range(row_tiles):
            for c in range(chunk_blocks):
                grad_ref[r, i * chunk_blocks + c] = grad[
                    r * sublanes:(r + 1) * sublanes, c * lanes:(c + 1) * lanes
                ]
        return carry

    lax.fori_loop(0, chunk_count, multiply, 0)
    pltpu.make_async_copy(tiles, tiles, tile_sem).wait()

    def pick(s, carry):
        block = index_s[0, s]
        row = block // row_blocks
        col = block - row * row_blocks
        mine = jnp.logical_and(sub == row % sublanes, s < count)
        held = tiles[s]
        grad = grad_ref[row // sublanes, col]
        grad_ref[row // sublanes, col] = jnp.where(mine, -held, grad)
        tiles[s] = jnp.where(mine, held + grad, 0.0)
        out_ref[0, pl.ds(s, 1), :] = tiles[s, pl.ds(row % sublanes, 1), :]
        return carry

    sub = lax.broadcasted_iota(jnp.int32, (sublanes, lanes), 0)

    lax.fori_loop(0, slots, pick, 0, unroll=8)
    message = out_ref[0]
    for j in range(1, members):
        out_ref[j] = message


def add_kernel(held, out_ref, *, slots):
    sources = held.shape[0]
    rows = out_ref.shape[0]
    base = lax.axis_index("grp") * rows
    target = (lax.broadcasted_iota(jnp.int32, (rows, lanes), 0) + base).astype(jnp.float32)
    low = lax.broadcasted_iota(jnp.int32, (1, lanes), 1) < slots
    total = jnp.zeros((rows, 2 * lanes), jnp.float32)
    for q in range(0, sources, 4):
        hits = []
        for p in (q, q + 2):
            code = jnp.where(low, held[p, slots:slots + 1, :], held[p + 1, slots:slots + 1, :])
            hits.append(jnp.where(target == code, 1.0, 0.0).astype(jnp.bfloat16))
        values = jnp.concatenate([held[p, 0:slots, :] for p in range(q, q + 4)], axis=0)
        high = values.astype(jnp.bfloat16)
        rest = (values - high.astype(jnp.float32)).astype(jnp.bfloat16)
        total = total + jnp.dot(
            jnp.concatenate(hits, axis=1),
            jnp.concatenate([high, rest], axis=1),
            preferred_element_type=jnp.float32,
        )
    out_ref[...] = total[:, :lanes] + total[:, lanes:]


def final_kernel(parts, momentum, out_ref):
    members, part, _ = out_ref.shape
    wide = part // sublanes * lanes
    me = lax.axis_index("grp")
    total = parts[0]
    for j in range(1, members):
        total = total + parts[j]
    rows = pl.ds(pl.multiple_of((me // 2) * sublanes, sublanes), sublanes)
    old = momentum[rows, pl.ds(pl.multiple_of((me % 2) * wide, lanes), wide)]
    for c in range(part // sublanes):
        at = slice(c * sublanes, (c + 1) * sublanes)
        new = momentum_decay * old[:, c * lanes:(c + 1) * lanes] + total[at]
        for j in range(members):
            out_ref[j, at, :] = new


def keep_kernel(grad, residual, out_ref):
    i = pl.program_id(0)
    for c in range(grad.shape[1]):
        at = slice(c * lanes, (c + 1) * lanes)
        out_ref[0, :, at] = residual[0, :, at] + grad[i, c]


def local(acts, grads_out, residual_in, sel_index, sel_count, momentum_in):
    tokens, width = acts.shape
    columns = grads_out.shape[1]
    slots = sel_index.shape[1]
    row_blocks = width // lanes
    own_blocks = momentum_in.shape[1] // lanes
    members = lax.axis_size("grp")
    owners = lax.axis_size("dev")
    part = own_blocks // 2 * sublanes
    smem = pl.BlockSpec(memory_space=pltpu.SMEM)
    vmem = pl.BlockSpec(memory_space=pltpu.VMEM)
    hbm = pl.BlockSpec(memory_space=pl.ANY)
    tiled = residual_in.reshape(columns // sublanes, sublanes, row_blocks, lanes)
    tiled = tiled.transpose(0, 2, 1, 3)

    def pick(*refs):
        pick_kernel(*refs, row_blocks=row_blocks, own_blocks=own_blocks)

    grad, message = pl.pallas_call(
        pick,
        in_specs=[smem, smem, vmem, vmem, hbm, hbm],
        out_specs=[vmem, vmem],
        out_shape=[
            pltpu.VMEM(tiled.shape, jnp.float32),
            pltpu.VMEM((members, slots + sublanes, lanes), jnp.float32),
        ],
        scratch_shapes=[
            pltpu.VMEM((chunk_count, tokens, width // chunk_count), jnp.bfloat16),
            pltpu.VMEM((slots, sublanes, lanes), jnp.float32),
            pltpu.VMEM((sublanes, lanes), jnp.float32),
            pltpu.SemaphoreType.DMA((chunk_count,)),
            pltpu.SemaphoreType.DMA,
        ],
        compiler_params=pltpu.CompilerParams(vmem_limit_bytes=16 << 20),
        name="pick",
    )(
        sel_index, sel_count, sel_index, grads_out.T,
        pltpu.with_memory_space_constraint(acts, pltpu.HBM),
        pltpu.with_memory_space_constraint(tiled, pltpu.HBM),
    )

    held = lax.all_to_all(message, "grp", 0, 0, tiled=True)

    sums = pl.pallas_call(
        lambda *refs: add_kernel(*refs, slots=slots),
        in_specs=[vmem],
        out_specs=vmem,
        out_shape=pltpu.VMEM((owners * part, lanes), jnp.float32),
        compiler_params=pltpu.CompilerParams(vmem_limit_bytes=8 << 20),
        name="add",
    )(held)
    parts = lax.all_to_all(sums.reshape(owners, part, lanes), "dev", 0, 0, tiled=True)

    new = pl.pallas_call(
        final_kernel,
        in_specs=[vmem, vmem],
        out_specs=vmem,
        out_shape=pltpu.VMEM((members, part, lanes), jnp.float32),
        compiler_params=pltpu.CompilerParams(vmem_limit_bytes=8 << 20),
        name="final",
    )(parts, momentum_in)
    whole = lax.all_to_all(new, "grp", 0, 0, tiled=True)
    whole = whole.reshape(columns // sublanes, 2, own_blocks // 2, sublanes, lanes)
    whole = whole.transpose(0, 3, 1, 2, 4).reshape(columns, own_blocks * lanes)
    block = pl.BlockSpec((1, sublanes, width), lambda i: (0, i, 0))
    kept = pl.pallas_call(
        keep_kernel,
        grid=(columns // sublanes,),
        in_specs=[vmem, block],
        out_specs=block,
        out_shape=jax.ShapeDtypeStruct(residual_in.shape, jnp.float32),
        compiler_params=pltpu.CompilerParams(vmem_limit_bytes=8 << 20),
        name="keep",
    )(
        pltpu.with_memory_space_constraint(grad, pltpu.VMEM),
        pltpu.with_memory_space_constraint(residual_in, pltpu.HBM),
    )
    return (kept, whole)


def solution(mesh):
    placed = (
        P(("grp", "dev"), None),
        P(("grp", "dev"), None),
        P(("grp", "dev"), None, None),
        P(("grp", "dev"), None),
        P(("grp", "dev")),
        P(None, "dev"),
    )
    return jax.shard_map(
        local,
        mesh=mesh,
        in_specs=placed,
        out_specs=(P(("grp", "dev"), None, None), P(None, "dev")),
        check_vma=False,
    )
```

time: 77 us -> 59.7 us (0.78)
  other arithmetic: 18.6 us -> 0 us
  blocking collectives: 25.6 us -> 39 us
  Pallas kernels: 0 us -> 12 us
  waiting for transfers between devices: 8.39 us -> 1.27 us
  starting transfers between devices: 10.6 us -> 3.52 us
  matrix products: 4.91 us -> 0 us
  local copies, waits for them, and re-layouts: 6.97 us -> 2.09 us
    all_to_all x0 -> x2, blocking collectives: none -> 39 us  [the longest x1 20.6 us: local(): lax.all_to_all(sums.reshape(owners, part, lanes), 'dev', 0, 0, tiled=True)]
    all_gather x1 -> x0, blocking collectives: 25.6 us -> none  [side_by_side(): filled, at, done = (lax.all_gather(both, axis, axis=dim, tiled=True), 0, [])]
    pallas_call x0 -> x4, Pallas kernels: none -> 12 us  [the longest x1 6.17 us: local(): pl.pallas_call(keep_kernel, grid=(columns // sublanes,), in_specs=[vmem,...]
    all_to_all x2 -> x1, waiting for transfers between devices: 8.39 us -> 1.27 us  [local(): whole = lax.all_to_all(new, 'grp', 0, 0, tiled=True)]
    all_to_all x2 -> x1, starting transfers between devices: 10.6 us -> 3.52 us  [local(): whole = lax.all_to_all(new, 'grp', 0, 0, tiled=True)]
    scatter-add x1 -> x0, other arithmetic: 7 us -> none  [local(): partial_sum = partial_sum.at[local_index].add(group_vals * owned[:, None])]
    mul x3 -> x0, other arithmetic: 5.61 us -> none  [the longest x1 3.64 us: local(): kept = (blocks * (1.0 - marked)[:, None]).reshape(1, columns, width)]
    dot_general x1 -> x0, matrix products: 4.91 us -> none  [local(): lax.dot_general(grads_out, acts, (((0,), (0,)), ((), ())), preferred_elem...]
  transfers between devices with their start and end apart: 2 -> 1, of which waited for: 2 -> 1; matrix products, arithmetic and copies ran while one was open for 7% -> 0% of each run, Pallas kernels for 0% -> 10%
where the time goes in v1:
time: 59.7 us; the launch traced here: 59.2 us
  blocking collectives  39 us (65%)
  Pallas kernels  12 us (20%)
  starting transfers between devices  3.52 us (6%)
  local copies, waits for them, and re-layouts  2.09 us (4%)
  between operations  1.31 us (2%)
  waiting for transfers between devices  1.27 us (2%)
    all_to_all x1, blocking collectives, local(): lax.all_to_all(sums.reshape(owners, part, lanes), 'dev', 0, 0, tiled=True)  20.6 us
    all_to_all x1, blocking collectives, local(): held = lax.all_to_all(message, 'grp', 0, 0, tiled=True)  18.5 us
    pallas_call x1, Pallas kernels, local(): pl.pallas_call(keep_kernel, grid=(columns // sublanes,), in_specs=[vmem,...  6.17 us
    pallas_call x1, Pallas kernels, local(): pl.pallas_call(pick, in_specs=[smem, smem, vmem, vmem, hbm, hbm], out_spe...  4.77 us
    all_to_all x1, starting transfers between devices, local(): whole = lax.all_to_all(new, 'grp', 0, 0, tiled=True)  3.52 us
    unnamed x7, local copies, waits for them, and re-layouts  2.09 us
    all_to_all x1, waiting for transfers between devices, local(): whole = lax.all_to_all(new, 'grp', 0, 0, tiled=True)  1.27 us
  transfers between devices with their start and end apart: 1, of which 1 were waited for; matrix products, arithmetic and copies ran while one was open for 0% of the time, Pallas kernels for 10%

profile of v1, /device:TPU:1, one launch (start us, length us, event | category | flops | bytes accessed | tf_op | source)
XLA Modules:
  0.0 59.2 jit_solution(12333449557614068838)
XLA Ops:
  1.3 0.0 copy-start.1
  1.3 0.7 %copy-done.1 = bf16[256,64]{0,1:T(8,128)(2,1)S(1)} copy-done((bf16[256,64]{0,1:T(8,128)(2,1)S(1)}, bf16[256,64]{0,1:T(8,128)(2,1)}, u32[]{:S(2)}) %copy-start.1) | copy-done | bytes 32792
  2.0 0.0 copy-start.2
  2.0 0.7 %copy-done.2 = s32[1,64]{1,0:T(1,128)S(1)} copy-done((s32[1,64]{1,0:T(1,128)S(1)}, s32[1,64]{1,0:T(1,128)}, u32[]{:S(2)}) %copy-start.2) | copy-done | bytes 280
  2.7 0.0 copy-start
  2.7 4.8 %pick.1 = (f32[8,96,8,128]{3,2,1,0:T(8,128)S(1)}, f32[16,72,128]{2,1,0:T(8,128)S(1)}) custom-call(s32[1,64]{1,0:T(1,128)S(1)} %copy-done.2, s32[1]{0:T(128)S(6)} %copy.9.refs_1_, s32[1,64]{1,0:T(1,128)S(1)} %copy-done.2, bf16[64,256]{1,0:T(8,128)(2,1)S(1)} %bitcast.11, bf16[256,12288]{1,0:T(8,128)(2,1)} %refs_4_.1, f32[8,96,8,128]{3,2,1,0:T(8,128)} %bitcast.12), custom_call_target="tpu_custom_call" | custom-call | tf_op jit(solution)/shard_map/pick/pallas_call | solution.py:155
  7.5 18.5 %all_to_all.15.refs_0_ = f32[16,72,128]{2,1,0:T(8,128)S(1)} all-to-all(f32[16,72,128]{2,1,0:T(8,128)S(1)} %get-tuple-element.5), channel_id=1, replica_groups=mesh['grp'=16,'dev'=16] {'grp'}, dimensions={0} | all-to-all | bytes 1179648 | tf_op jit(solution)/shard_map/all_to_all | solution.py:178
  25.9 0.4 add.1
  26.3 20.6 %all_to_all.16.parts = f32[16,24,128]{2,1,0:T(8,128)S(1)} all-to-all(f32[16,24,128]{2,1,0:T(8,128)S(1)} %bitcast.10), channel_id=1, replica_groups=mesh['grp'=16,'dev'=16] {'dev'}, dimensions={0} | all-to-all | bytes 393216 | tf_op jit(solution)/shard_map/all_to_all | solution.py:188
  46.9 0.0 copy-done
  46.9 0.7 %final.1 = f32[16,24,128]{2,1,0:T(8,128)} custom-call(f32[16,24,128]{2,1,0:T(8,128)S(1)} %all_to_all.16.parts, f32[64,768]{1,0:T(8,128)S(1)} %copy-done), custom_call_target="tpu_custom_call" | custom-call | tf_op jit(solution)/shard_map/final/pallas_call | solution.py:190
  47.6 3.5 %all-to-all-start.2 = ((f32[16,24,128]{2,1,0:T(8,128)}), f32[16,24,128]{2,1,0:T(8,128)S(1)}, u32[]{:S(2)}, u32[]{:S(2)}) async-start(f32[16,24,128]{2,1,0:T(8,128)} %final.1), calls=%async_computation.2 | async-start | bytes 393216 | tf_op jit(solution)/shard_map/all_to_all | solution.py:198
  51.1 6.2 %keep.1 = f32[1,64,12288]{2,1,0:T(8,128)} custom-call(f32[8,96,8,128]{3,2,1,0:T(8,128)S(1)} %get-tuple-element.4.grad, f32[1,64,12288]{2,1,0:T(8,128)} %residual.1), custom_call_target="tpu_custom_call" | custom-call | tf_op jit(solution)/shard_map/keep/pallas_call | solution.py:202
  57.3 1.3 %all-to-all-done.2 = f32[16,24,128]{2,1,0:T(8,128)S(1)} async-done(((f32[16,24,128]{2,1,0:T(8,128)}), f32[16,24,128]{2,1,0:T(8,128)S(1)}, u32[]{:S(2)}, u32[]{:S(2)}) %all-to-all-start.2) | async-done | bytes 196640 | tf_op jit(solution)/shard_map/all_to_all | solution.py:198
  58.6 0.7 %copy.10 = f32[64,768]{1,0:T(8,128)} copy(f32[64,768]{1,0:T(8,128)S(1)} %bitcast.13) | data formatting | bytes 393216
Async XLA Ops:
  1.3 0.8 %copy-start.1 = (bf16[256,64]{0,1:T(8,128)(2,1)S(1)}, bf16[256,64]{0,1:T(8,128)(2,1)}, u32[]{:S(2)}) copy-start(bf16[256,64]{0,1:T(8,128)(2,1)} %param.7) | copy-start | bytes 98308
  2.0 0.7 %copy-start.2 = (s32[1,64]{1,0:T(1,128)S(1)}, s32[1,64]{1,0:T(1,128)}, u32[]{:S(2)}) copy-start(s32[1,64]{1,0:T(1,128)} %refs_2_.1) | copy-start | bytes 772
  2.7 44.2 %copy-start = (f32[64,768]{1,0:T(8,128)S(1)}, f32[64,768]{1,0:T(8,128)}, u32[]{:S(2)}) copy-start(f32[64,768]{1,0:T(8,128)} %momentum.1) | copy-start | bytes 589828
  47.6 11.0 %all-to-all-start.2 = ((f32[16,24,128]{2,1,0:T(8,128)}), f32[16,24,128]{2,1,0:T(8,128)S(1)}, u32[]{:S(2)}, u32[]{:S(2)}) async-start(f32[16,24,128]{2,1,0:T(8,128)} %final.1), calls=%async_computation.2 | async-start | bytes 393216 | tf_op jit(solution)/shard_map/all_to_all | solution.py:198

commit v2 on v1

--- a/solution.py
+++ b/solution.py
@@ -8,36 +8,53 @@
 momentum_decay = 0.9
 lanes = 128
 sublanes = 8
-chunk_count = 8
-
-
-def pick_kernel(index_s, count_s, index_v, grads_t, acts, residual, grad_ref, out_ref,
-                acts_v, tiles, codes_v, acts_sems, tile_sem, *, row_blocks, own_blocks):
+chunk_count = 3
+
+
+def pick_kernel(index, count_s, grads_t, acts, residual, grad_ref, out_ref,
+                index_s, index_v, grads_v, acts_v, tiles, codes_v,
+                small_sems, acts_sems, tile_sem, *, row_blocks, own_blocks):
     row_tiles = grad_ref.shape[0]
-    slots = index_s.shape[1]
-    chunk = row_blocks * lanes // chunk_count
-    chunk_blocks = row_blocks // chunk_count
+    slots = index.shape[1]
     members = out_ref.shape[0]
     half = own_blocks // 2
     part = half * sublanes
-
-    def acts_copy(i):
-        at = pl.ds(pl.multiple_of(i * chunk, lanes), chunk)
-        return pltpu.make_async_copy(acts.at[:, at], acts_v.at[i], acts_sems.at[i])
-
-    for i in range(chunk_count):
-        acts_copy(i).start()
-
-    def fetch(s, carry):
+    chunk_blocks = row_blocks // chunk_count
+    chunk = chunk_blocks * lanes
+
+    scalars = pltpu.make_async_copy(index, index_s, small_sems.at[0])
+    vector = pltpu.make_async_copy(index, index_v, small_sems.at[1])
+    left = pltpu.make_async_copy(grads_t, grads_v, small_sems.at[2])
+    chunks = [
+        pltpu.make_async_copy(
+            acts.at[:, i * chunk:(i + 1) * chunk],
+            acts_v.at[:, i * chunk:(i + 1) * chunk],
+            acts_sems.at[i],
+        )
+        for i in range(chunk_count)
+    ]
+    scalars.start()
+    left.start()
+    chunks[0].start()
+    vector.start()
+    for copy in chunks[1:]:
+        copy.start()
+
+    def place(s):
         block = index_s[0, s]
         row = block // row_blocks
-        col = block - row * row_blocks
-        pltpu.make_async_copy(residual.at[row // sublanes, col], tiles.at[s], tile_sem).start()
+        return row // sublanes, row % sublanes, block - row * row_blocks
+
+    def fetch(s, carry):
+        high, _, col = place(s)
+        pltpu.make_async_copy(residual.at[high, col], tiles.at[s], tile_sem).start()
         return carry
 
+    scalars.wait()
     lax.fori_loop(0, slots, fetch, 0, unroll=8)
 
     count = count_s[0]
+    vector.wait()
     block = index_v[...]
     row = (block * 43691) >> 22
     col = block - row * row_blocks
@@ -55,32 +72,32 @@
     both = both + pltpu.roll(both, slots, 1)
     out_ref[0, slots:slots + sublanes, :] = both
 
-    def multiply(i, carry):
-        acts_copy(i).wait()
-        grad = jnp.dot(grads_t[...], acts_v[i], preferred_element_type=jnp.float32)
+    left.wait()
+    for i in range(chunk_count):
+        chunks[i].wait()
+        grad = jnp.dot(
+            grads_v[...],
+            acts_v[:, i * chunk:(i + 1) * chunk],
+            preferred_element_type=jnp.float32,
+        )
         for r in range(row_tiles):
             for c in range(chunk_blocks):
                 grad_ref[r, i * chunk_blocks + c] = grad[
                     r * sublanes:(r + 1) * sublanes, c * lanes:(c + 1) * lanes
                 ]
+    pltpu.make_async_copy(tiles, tiles, tile_sem).wait()
+
+    sub = lax.broadcasted_iota(jnp.int32, (sublanes, lanes), 0)
+
+    def pick(s, carry):
+        high, low, col = place(s)
+        mine = jnp.logical_and(sub == low, s < count)
+        held = tiles[s]
+        grad = grad_ref[high, col]
+        grad_ref[high, col] = jnp.where(mine, -held, grad)
+        tiles[s] = jnp.where(mine, held + grad, 0.0)
+        out_ref[0, pl.ds(s, 1), :] = tiles[s, pl.ds(low, 1), :]
         return carry
-
-    lax.fori_loop(0, chunk_count, multiply, 0)
-    pltpu.make_async_copy(tiles, tiles, tile_sem).wait()
-
-    def pick(s, carry):
-        block = index_s[0, s]
-        row = block // row_blocks
-        col = block - row * row_blocks
-        mine = jnp.logical_and(sub == row % sublanes, s < count)
-        held = tiles[s]
-        grad = grad_ref[row // sublanes, col]
-        grad_ref[row // sublanes, col] = jnp.where(mine, -held, grad)
-        tiles[s] = jnp.where(mine, held + grad, 0.0)
-        out_ref[0, pl.ds(s, 1), :] = tiles[s, pl.ds(row % sublanes, 1), :]
-        return carry
-
-    sub = lax.broadcasted_iota(jnp.int32, (sublanes, lanes), 0)
 
     lax.fori_loop(0, slots, pick, 0, unroll=8)
     message = out_ref[0]
@@ -127,11 +144,33 @@
             out_ref[j, at, :] = new
 
 
-def keep_kernel(grad, residual, out_ref):
-    i = pl.program_id(0)
-    for c in range(grad.shape[1]):
-        at = slice(c * lanes, (c + 1) * lanes)
-        out_ref[0, :, at] = residual[0, :, at] + grad[i, c]
+def keep_kernel(grad, residual, out_ref, held, in_sems, out_sems):
+    row_tiles, row_blocks, _, _ = grad.shape
+    reads = [
+        pltpu.make_async_copy(residual.at[i], held.at[i], in_sems.at[i])
+        for i in range(row_tiles)
+    ]
+    writes = [
+        pltpu.make_async_copy(held.at[i], out_ref.at[i], out_sems.at[i])
+        for i in range(row_tiles)
+    ]
+    for copy in reads:
+        copy.start()
+    for i in range(row_tiles):
+        reads[i].wait()
+
+        def add(c, carry):
+            held[i, c] = held[i, c] + grad[i, c]
+            return carry
+
+        lax.fori_loop(0, row_blocks, add, 0, unroll=16)
+        writes[i].start()
+    for copy in writes:
+        copy.wait()
+
+
+def in_hbm(array):
+    return pltpu.with_memory_space_constraint(array, pltpu.HBM)
 
 
 def local(acts, grads_out, residual_in, sel_index, sel_count, momentum_in):
@@ -154,25 +193,27 @@
 
     grad, message = pl.pallas_call(
         pick,
-        in_specs=[smem, smem, vmem, vmem, hbm, hbm],
+        in_specs=[hbm, smem, hbm, hbm, hbm],
         out_specs=[vmem, vmem],
         out_shape=[
             pltpu.VMEM(tiled.shape, jnp.float32),
             pltpu.VMEM((members, slots + sublanes, lanes), jnp.float32),
         ],
         scratch_shapes=[
-            pltpu.VMEM((chunk_count, tokens, width // chunk_count), jnp.bfloat16),
+            pltpu.SMEM((1, slots), jnp.int32),
+            pltpu.VMEM((1, slots), jnp.int32),
+            pltpu.VMEM((columns, tokens), jnp.bfloat16),
+            pltpu.VMEM((tokens, width), jnp.bfloat16),
             pltpu.VMEM((slots, sublanes, lanes), jnp.float32),
             pltpu.VMEM((sublanes, lanes), jnp.float32),
+            pltpu.SemaphoreType.DMA((3,)),
             pltpu.SemaphoreType.DMA((chunk_count,)),
             pltpu.SemaphoreType.DMA,
         ],
         compiler_params=pltpu.CompilerParams(vmem_limit_bytes=16 << 20),
         name="pick",
     )(
-        sel_index, sel_count, sel_index, grads_out.T,
-        pltpu.with_memory_space_constraint(acts, pltpu.HBM),
-        pltpu.with_memory_space_constraint(tiled, pltpu.HBM),
+        in_hbm(sel_index), sel_count, in_hbm(grads_out.T), in_hbm(acts), in_hbm(tiled),
     )
 
     held = lax.all_to_all(message, "grp", 0, 0, tiled=True)
@@ -198,19 +239,20 @@
     whole = lax.all_to_all(new, "grp", 0, 0, tiled=True)
     whole = whole.reshape(columns // sublanes, 2, own_blocks // 2, sublanes, lanes)
     whole = whole.transpose(0, 3, 1, 2, 4).reshape(columns, own_blocks * lanes)
-    block = pl.BlockSpec((1, sublanes, width), lambda i: (0, i, 0))
     kept = pl.pallas_call(
         keep_kernel,
-        grid=(columns // sublanes,),
-        in_specs=[vmem, block],
-        out_specs=block,
-        out_shape=jax.ShapeDtypeStruct(residual_in.shape, jnp.float32),
+        in_specs=[vmem, hbm],
+        out_specs=hbm,
+        out_shape=pltpu.HBM(tiled.shape, jnp.float32),
+        scratch_shapes=[
+            pltpu.VMEM(tiled.shape, jnp.float32),
+            pltpu.SemaphoreType.DMA((tiled.shape[0],)),
+            pltpu.SemaphoreType.DMA((tiled.shape[0],)),
+        ],
         compiler_params=pltpu.CompilerParams(vmem_limit_bytes=8 << 20),
         name="keep",
-    )(
-        pltpu.with_memory_space_constraint(grad, pltpu.VMEM),
-        pltpu.with_memory_space_constraint(residual_in, pltpu.HBM),
-    )
+    )(pltpu.with_memory_space_constraint(grad, pltpu.VMEM), in_hbm(tiled))
+    kept = kept.transpose(0, 2, 1, 3).reshape(residual_in.shape)
     return (kept, whole)
 
 

time: 59.7 us -> 57.9 us (0.970)
  Pallas kernels: 12 us -> 8.47 us
  waiting for transfers between devices: 1.27 us -> 4.59 us
  local copies, waits for them, and re-layouts: 2.09 us -> 0.68 us
    pallas_call x2, Pallas kernels: 10.9 us -> 7.39 us  [the longest x1 4.55 us: local(): pl.pallas_call(pick, in_specs=[hbm, smem, hbm, hbm, hbm], out_specs=[vmem...]
    all_to_all x1, waiting for transfers between devices: 1.27 us -> 4.59 us  [local(): whole = lax.all_to_all(new, 'grp', 0, 0, tiled=True)]
    unnamed x7 -> x3, local copies, waits for them, and re-layouts: 2.09 us -> 0.68 us
  transfers between devices with their start and end apart: 1 -> 1, of which waited for: 1 -> 1; matrix products, arithmetic and copies ran while one was open for 0% -> 0% of each run, Pallas kernels for 10% -> 5%
where the time goes in v2:
time: 57.9 us; the launch traced here: 57.6 us
  blocking collectives  39 us (67%)
  Pallas kernels  8.47 us (15%)
  waiting for transfers between devices  4.59 us (8%)
  starting transfers between devices  3.52 us (6%)
  between operations  1.32 us (2%)
  local copies, waits for them, and re-layouts  0.68 us (1%)
    all_to_all x1, blocking collectives, local(): lax.all_to_all(sums.reshape(owners, part, lanes), 'dev', 0, 0, tiled=True)  20.6 us
    all_to_all x1, blocking collectives, local(): held = lax.all_to_all(message, 'grp', 0, 0, tiled=True)  18.5 us
    all_to_all x1, waiting for transfers between devices, local(): whole = lax.all_to_all(new, 'grp', 0, 0, tiled=True)  4.59 us
    pallas_call x1, Pallas kernels, local(): pl.pallas_call(pick, in_specs=[hbm, smem, hbm, hbm, hbm], out_specs=[vmem...  4.55 us
    all_to_all x1, starting transfers between devices, local(): whole = lax.all_to_all(new, 'grp', 0, 0, tiled=True)  3.52 us
    pallas_call x1, Pallas kernels, local(): pl.pallas_call(keep_kernel, in_specs=[vmem, hbm], out_specs=hbm, out_shap...  2.84 us
  transfers between devices with their start and end apart: 1, of which 1 were waited for; matrix products, arithmetic and copies ran while one was open for 0% of the time, Pallas kernels for 5%

profile of v2, /device:TPU:1, one launch (start us, length us, event | category | flops | bytes accessed | tf_op | source)
XLA Modules:
  0.0 57.6 jit_solution(17545699738514674305)
XLA Ops:
  1.3 0.0 copy-start
  1.3 4.5 %pick.1 = (f32[8,96,8,128]{3,2,1,0:T(8,128)S(1)}, f32[16,72,128]{2,1,0:T(8,128)S(1)}) custom-call(s32[1,64]{1,0:T(1,128)} %refs_0_.1, s32[1]{0:T(128)S(6)} %copy.9.refs_1_, bf16[64,256]{1,0:T(8,128)(2,1)} %bitcast.18, bf16[256,12288]{1,0:T(8,128)(2,1)} %refs_3_.1, f32[8,96,8,128]{3,2,1,0:T(8,128)} %bitcast.14), custom_call_target="tpu_custom_call" | custom-call | tf_op jit(solution)/shard_map/pick/pallas_call | solution.py:194
  5.8 18.5 %all_to_all.15.refs_0_ = f32[16,72,128]{2,1,0:T(8,128)S(1)} all-to-all(f32[16,72,128]{2,1,0:T(8,128)S(1)} %get-tuple-element.5), channel_id=1, replica_groups=mesh['grp'=16,'dev'=16] {'grp'}, dimensions={0} | all-to-all | bytes 1179648 | tf_op jit(solution)/shard_map/all_to_all | solution.py:219
  24.3 0.4 add.1
  24.7 20.6 %all_to_all.16.parts = f32[16,24,128]{2,1,0:T(8,128)S(1)} all-to-all(f32[16,24,128]{2,1,0:T(8,128)S(1)} %bitcast.13), channel_id=1, replica_groups=mesh['grp'=16,'dev'=16] {'dev'}, dimensions={0} | all-to-all | bytes 393216 | tf_op jit(solution)/shard_map/all_to_all | solution.py:229
  45.2 0.0 copy-done
  45.2 0.7 %final.1 = f32[16,24,128]{2,1,0:T(8,128)} custom-call(f32[16,24,128]{2,1,0:T(8,128)S(1)} %all_to_all.16.parts, f32[64,768]{1,0:T(8,128)S(1)} %copy-done), custom_call_target="tpu_custom_call" | custom-call | tf_op jit(solution)/shard_map/final/pallas_call | solution.py:231
  46.0 3.5 %all-to-all-start.2 = ((f32[16,24,128]{2,1,0:T(8,128)}), f32[16,24,128]{2,1,0:T(8,128)S(1)}, u32[]{:S(2)}, u32[]{:S(2)}) async-start(f32[16,24,128]{2,1,0:T(8,128)} %final.1), calls=%async_computation.2 | async-start | bytes 393216 | tf_op jit(solution)/shard_map/all_to_all | solution.py:239
  49.5 2.8 %keep.1 = f32[8,96,8,128]{3,2,1,0:T(8,128)} custom-call(f32[8,96,8,128]{3,2,1,0:T(8,128)S(1)} %get-tuple-element.4.grad, f32[8,96,8,128]{3,2,1,0:T(8,128)} %bitcast.15), custom_call_target="tpu_custom_call" | custom-call | tf_op jit(solution)/shard_map/keep/pallas_call | solution.py:242
  52.3 4.6 %all-to-all-done.2 = f32[16,24,128]{2,1,0:T(8,128)S(1)} async-done(((f32[16,24,128]{2,1,0:T(8,128)}), f32[16,24,128]{2,1,0:T(8,128)S(1)}, u32[]{:S(2)}, u32[]{:S(2)}) %all-to-all-start.2) | async-done | bytes 196640 | tf_op jit(solution)/shard_map/all_to_all | solution.py:239
  56.9 0.7 %copy.10 = f32[64,768]{1,0:T(8,128)} copy(f32[64,768]{1,0:T(8,128)S(1)} %bitcast.17) | data formatting | bytes 393216
Async XLA Ops:
  1.3 44.0 %copy-start = (f32[64,768]{1,0:T(8,128)S(1)}, f32[64,768]{1,0:T(8,128)}, u32[]{:S(2)}) copy-start(f32[64,768]{1,0:T(8,128)} %momentum.1) | copy-start | bytes 589828
  46.0 11.0 %all-to-all-start.2 = ((f32[16,24,128]{2,1,0:T(8,128)}), f32[16,24,128]{2,1,0:T(8,128)S(1)}, u32[]{:S(2)}, u32[]{:S(2)}) async-start(f32[16,24,128]{2,1,0:T(8,128)} %final.1), calls=%async_computation.2 | async-start | bytes 393216 | tf_op jit(solution)/shard_map/all_to_all | solution.py:239

commit v3 on v2

v3 whole, which is shorter than its diff:
```python
import jax
import jax.numpy as jnp
from jax import lax
from jax.experimental import pallas as pl
from jax.experimental.pallas import tpu as pltpu
from jax.sharding import Mesh
from jax.sharding import PartitionSpec as P

momentum_decay = 0.9
lanes = 128
sublanes = 8
chunk_count = 3


def pick_kernel(index, count_s, grads_t, acts, residual, kept_ref, out_ref,
                index_s, index_v, grads_v, acts_v, residual_v, codes_v,
                small_sems, acts_sems, residual_sems, *, row_blocks, own_blocks):
    row_tiles = kept_ref.shape[0]
    slots = index.shape[1]
    rows = slots + 1
    members = out_ref.shape[0] // rows
    half = own_blocks // 2
    part = half * sublanes
    chunk_blocks = row_blocks // chunk_count
    chunk = chunk_blocks * lanes

    scalars = pltpu.make_async_copy(index, index_s, small_sems.at[0])
    vector = pltpu.make_async_copy(index, index_v, small_sems.at[1])
    left = pltpu.make_async_copy(grads_t, grads_v, small_sems.at[2])
    chunks = [
        pltpu.make_async_copy(
            acts.at[:, i * chunk:(i + 1) * chunk],
            acts_v.at[:, i * chunk:(i + 1) * chunk],
            acts_sems.at[i],
        )
        for i in range(chunk_count)
    ]
    addends = [
        pltpu.make_async_copy(
            residual.at[:, i * chunk_blocks:(i + 1) * chunk_blocks],
            residual_v.at[:, i * chunk_blocks:(i + 1) * chunk_blocks],
            residual_sems.at[i],
        )
        for i in range(chunk_count)
    ]
    left.start()
    chunks[0].start()
    vector.start()
    scalars.start()
    for i in range(chunk_count):
        if i + 1 < chunk_count:
            chunks[i + 1].start()
        addends[i].start()

    count = count_s[0]
    vector.wait()
    block = index_v[...]
    row = (block * 43691) >> 22
    col = block - row * row_blocks
    owner = (col * 10923) >> 16
    inner = col - owner * own_blocks
    side = jnp.where(inner >= half, 1, 0)
    share = (row >> 3) * 2 + side
    target = owner * part + (inner - side * half) * sublanes + (row & 7)
    code = share * (part * row_blocks // own_blocks) + target
    slot = lax.broadcasted_iota(jnp.int32, code.shape, 1)
    code = jnp.where(slot < count, code, -1).astype(jnp.float32)
    codes_v[...] = jnp.zeros_like(codes_v)
    codes_v[0:1, 0:slots] = code
    both = codes_v[...]
    both = both + pltpu.roll(both, slots, 1)
    out_ref[slots:rows, :] = both[0:1]

    left.wait()
    for i in range(chunk_count):
        chunks[i].wait()
        grad = jnp.dot(
            grads_v[...],
            acts_v[:, i * chunk:(i + 1) * chunk],
            preferred_element_type=jnp.float32,
        )
        addends[i].wait()
        for r in range(row_tiles):
            for c in range(chunk_blocks):
                at = i * chunk_blocks + c
                kept_ref[r, at] = residual_v[r, at] + grad[
                    r * sublanes:(r + 1) * sublanes, c * lanes:(c + 1) * lanes
                ]

    scalars.wait()
    sub = lax.broadcasted_iota(jnp.int32, (sublanes, lanes), 0)

    def pick(s, carry):
        block = index_s[0, s]
        row = block // row_blocks
        high, low, col = row // sublanes, row % sublanes, block - row * row_blocks
        out_ref[pl.ds(s, 1), :] = kept_ref[high, col, pl.ds(low, 1), :]
        mine = jnp.logical_and(sub == low, s < count)
        kept_ref[high, col] = jnp.where(mine, 0.0, kept_ref[high, col])
        return carry

    lax.fori_loop(0, slots, pick, 0, unroll=8)
    message = out_ref[0:rows, :]
    for j in range(1, members):
        out_ref[j * rows:(j + 1) * rows, :] = message


def add_kernel(held, own_ref, other_ref, *, slots, rows):
    step = slots + 1
    sources = held.shape[0] // step
    base = lax.axis_index("grp") * rows
    target = (lax.broadcasted_iota(jnp.int32, (rows, lanes), 0) + base).astype(jnp.float32)
    low = lax.broadcasted_iota(jnp.int32, (1, lanes), 1) < slots
    total = jnp.zeros((rows, 2 * lanes), jnp.float32)
    for q in range(0, sources, 4):
        hits = []
        for p in (q, q + 2):
            code = jnp.where(
                low,
                held[p * step + slots:(p + 1) * step, :],
                held[(p + 1) * step + slots:(p + 2) * step, :],
            )
            hits.append(jnp.where(target == code, 1.0, 0.0).astype(jnp.bfloat16))
        values = jnp.concatenate([held[p * step:p * step + slots, :] for p in range(q, q + 4)], axis=0)
        high = values.astype(jnp.bfloat16)
        rest = (values - high.astype(jnp.float32)).astype(jnp.bfloat16)
        total = total + jnp.dot(
            jnp.concatenate(hits, axis=1),
            jnp.concatenate([high, rest], axis=1),
            preferred_element_type=jnp.float32,
        )
    total = total[:, :lanes] + total[:, lanes:]
    part = rows // (2 * own_ref.shape[0])
    second = lax.axis_index("core") == 1
    for z in range(own_ref.shape[0]):
        even = total[2 * z * part:(2 * z + 1) * part]
        odd = total[(2 * z + 1) * part:(2 * z + 2) * part]
        own_ref[z] = jnp.where(second, odd, even)
        other_ref[z] = jnp.where(second, even, odd)


def store_kernel(kept, out_ref, sems):
    copies = [
        pltpu.make_async_copy(kept.at[i], out_ref.at[i], sems.at[i])
        for i in range(kept.shape[0])
    ]
    for copy in copies:
        copy.start()
    for copy in copies:
        copy.wait()


def join_kernel(own, other, stored, out_ref):
    out_ref[...] = own[...] + other[...]


def final_kernel(parts, momentum, out_ref):
    members, part, _ = out_ref.shape
    wide = part // sublanes * lanes
    me = lax.axis_index("grp")
    total = parts[0]
    for j in range(1, parts.shape[0]):
        total = total + parts[j]
    rows = pl.ds(pl.multiple_of((me // 2) * sublanes, sublanes), sublanes)
    old = momentum[rows, pl.ds(pl.multiple_of((me % 2) * wide, lanes), wide)]
    for c in range(part // sublanes):
        at = slice(c * sublanes, (c + 1) * sublanes)
        new = momentum_decay * old[:, c * lanes:(c + 1) * lanes] + total[at]
        for j in range(members):
            out_ref[j, at, :] = new


def in_hbm(array):
    return pltpu.with_memory_space_constraint(array, pltpu.HBM)


def local(acts, grads_out, residual_in, sel_index, sel_count, momentum_in):
    tokens, width = acts.shape
    columns = grads_out.shape[1]
    slots = sel_index.shape[1]
    row_blocks = width // lanes
    own_blocks = momentum_in.shape[1] // lanes
    members = lax.axis_size("grp")
    owners = lax.axis_size("z") * lax.axis_size("core")
    part = own_blocks // 2 * sublanes
    smem = pl.BlockSpec(memory_space=pltpu.SMEM)
    vmem = pl.BlockSpec(memory_space=pltpu.VMEM)
    hbm = pl.BlockSpec(memory_space=pl.ANY)
    tiled = residual_in.reshape(columns // sublanes, sublanes, row_blocks, lanes)
    tiled = tiled.transpose(0, 2, 1, 3)

    def pick(*refs):
        pick_kernel(*refs, row_blocks=row_blocks, own_blocks=own_blocks)

    kept, message = pl.pallas_call(
        pick,
        in_specs=[hbm, smem, hbm, hbm, hbm],
        out_specs=[vmem, vmem],
        out_shape=[
            pltpu.VMEM(tiled.shape, jnp.float32),
            pltpu.VMEM((members * (slots + 1), lanes), jnp.float32),
        ],
        scratch_shapes=[
            pltpu.SMEM((1, slots), jnp.int32),
            pltpu.VMEM((1, slots), jnp.int32),
            pltpu.VMEM((columns, tokens), jnp.bfloat16),
            pltpu.VMEM((tokens, width), jnp.bfloat16),
            pltpu.VMEM(tiled.shape, jnp.float32),
            pltpu.VMEM((sublanes, lanes), jnp.float32),
            pltpu.SemaphoreType.DMA((3,)),
            pltpu.SemaphoreType.DMA((chunk_count,)),
            pltpu.SemaphoreType.DMA((chunk_count,)),
        ],
        compiler_params=pltpu.CompilerParams(vmem_limit_bytes=16 << 20),
        name="pick",
    )(
        in_hbm(sel_index), sel_count, in_hbm(grads_out.T), in_hbm(acts), in_hbm(tiled),
    )

    held = lax.all_to_all(
        message.reshape(members, slots + 1, 1, lanes), "grp", 0, 0, tiled=True
    ).reshape(message.shape)

    shape = (lax.axis_size("z"), part, lanes)
    own, other = pl.pallas_call(
        lambda *refs: add_kernel(*refs, slots=slots, rows=owners * part),
        in_specs=[vmem],
        out_specs=[vmem, vmem],
        out_shape=[pltpu.VMEM(shape, jnp.float32), pltpu.VMEM(shape, jnp.float32)],
        compiler_params=pltpu.CompilerParams(vmem_limit_bytes=8 << 20),
        name="add",
    )(held)
    other = lax.ppermute(other, "core", [(0, 1), (1, 0)])
    kept = pl.pallas_call(
        store_kernel,
        in_specs=[vmem],
        out_specs=hbm,
        out_shape=pltpu.HBM(tiled.shape, jnp.float32),
        scratch_shapes=[pltpu.SemaphoreType.DMA((tiled.shape[0],))],
        compiler_params=pltpu.CompilerParams(vmem_limit_bytes=8 << 20),
        name="store",
    )(kept)
    sums = pl.pallas_call(
        join_kernel,
        in_specs=[vmem, vmem, hbm],
        out_specs=vmem,
        out_shape=pltpu.VMEM(shape, jnp.float32),
        compiler_params=pltpu.CompilerParams(vmem_limit_bytes=8 << 20),
        name="join",
    )(own, other, in_hbm(kept))
    parts = lax.all_to_all(sums, "z", 0, 0, tiled=True)

    new = pl.pallas_call(
        final_kernel,
        in_specs=[vmem, vmem],
        out_specs=vmem,
        out_shape=pltpu.VMEM((members, part, lanes), jnp.float32),
        compiler_params=pltpu.CompilerParams(vmem_limit_bytes=8 << 20),
        name="final",
    )(parts, momentum_in)
    whole = lax.all_to_all(new, "grp", 0, 0, tiled=True)
    whole = whole.reshape(columns // sublanes, 2, own_blocks // 2, sublanes, lanes)
    whole = whole.transpose(0, 3, 1, 2, 4).reshape(columns, own_blocks * lanes)
    kept = kept.transpose(0, 2, 1, 3).reshape(residual_in.shape)
    return (kept, whole)


def solution(mesh):
    groups, devices = mesh.devices.shape
    split = Mesh(mesh.devices.reshape(groups, devices // 2, 2), ("grp", "z", "core"))
    every = ("grp", "z", "core")
    owner = ("z", "core")
    placed = (
        P(every, None),
        P(every, None),
        P(every, None, None),
        P(every, None),
        P(every),
        P(None, owner),
    )
    return jax.shard_map(
        local,
        mesh=split,
        in_specs=placed,
        out_specs=(P(every, None, None), P(None, owner)),
        check_vma=False,
    )
```

time: 57.9 us -> 55.9 us (0.965)
  blocking collectives: 39 us -> 44 us
  waiting for transfers between devices: 4.59 us -> 0.01 us
  starting transfers between devices: 3.52 us -> 1.94 us
  Pallas kernels: 8.47 us -> 7.3 us
    all_to_all x2 -> x3, blocking collectives: 39 us -> 44 us  [the longest x1 18.3 us: local(): lax.all_to_all(message.reshape(members, slots + 1, 1, lanes), 'grp', 0, 0...]
    all_to_all x1 -> x0, waiting for transfers between devices: 4.59 us -> none  [local(): whole = lax.all_to_all(new, 'grp', 0, 0, tiled=True)]
    all_to_all x1 -> x0, starting transfers between devices: 3.52 us -> none  [local(): whole = lax.all_to_all(new, 'grp', 0, 0, tiled=True)]
    ppermute x0 -> x1, starting transfers between devices: none -> 1.94 us  [local(): other = lax.ppermute(other, 'core', [(0, 1), (1, 0)])]
    pallas_call x2 -> x3, Pallas kernels: 3.21 us -> 2.11 us  [the longest x1 1.72 us: local(): pl.pallas_call(store_kernel, in_specs=[vmem], out_specs=hbm, out_shape=pl...]
    pallas_call x1, Pallas kernels: 0.71 us -> 0.03 us  [local(): pl.pallas_call(final_kernel, in_specs=[vmem, vmem], out_specs=vmem, out_s...]
    pallas_call x1, Pallas kernels: 4.55 us -> 5.16 us  [local(): pl.pallas_call(pick, in_specs=[hbm, smem, hbm, hbm, hbm], out_specs=[vmem...]
  transfers between devices with their start and end apart: 1 -> 1, of which waited for: 1 -> 0; matrix products, arithmetic and copies ran while one was open for 0% -> 0% of each run, Pallas kernels for 5% -> 3%
where the time goes in v3:
time: 55.9 us; the launch traced here: 55.3 us
  blocking collectives  44 us (79%)
  Pallas kernels  7.3 us (13%)
  starting transfers between devices  1.94 us (3%)
  between operations  1.33 us (2%)
  local copies, waits for them, and re-layouts  0.68 us (1%)
    all_to_all x1, blocking collectives, local(): lax.all_to_all(message.reshape(members, slots + 1, 1, lanes), 'grp', 0, 0...  18.3 us
    all_to_all x1, blocking collectives, local(): parts = lax.all_to_all(sums, 'z', 0, 0, tiled=True)  15.9 us
    all_to_all x1, blocking collectives, local(): whole = lax.all_to_all(new, 'grp', 0, 0, tiled=True)  9.87 us
    pallas_call x1, Pallas kernels, local(): pl.pallas_call(pick, in_specs=[hbm, smem, hbm, hbm, hbm], out_specs=[vmem...  5.16 us
    ppermute x1, starting transfers between devices, local(): other = lax.ppermute(other, 'core', [(0, 1), (1, 0)])  1.94 us
    pallas_call x1, Pallas kernels, local(): pl.pallas_call(store_kernel, in_specs=[vmem], out_specs=hbm, out_shape=pl...  1.72 us
  transfers between devices with their start and end apart: 1, of which 0 were waited for; matrix products, arithmetic and copies ran while one was open for 0% of the time, Pallas kernels for 3%

profile of v3, /device:TPU:1, one launch (start us, length us, event | category | flops | bytes accessed | tf_op | source)
XLA Modules:
  0.0 55.3 jit_solution(7355293616202547842)
XLA Ops:
  1.3 5.2 %pick.1 = (f32[8,96,8,128]{3,2,1,0:T(8,128)S(1)}, f32[1040,128]{1,0:T(8,128)S(1)}) custom-call(s32[1,64]{1,0:T(1,128)} %refs_0_.1, s32[1]{0:T(128)S(6)} %copy.10.refs_1_, bf16[64,256]{1,0:T(8,128)(2,1)} %bitcast.19, bf16[256,12288]{1,0:T(8,128)(2,1)} %refs_3_.1, f32[8,96,8,128]{3,2,1,0:T(8,128)} %bitcast.17), custom_call_target="tpu_custom_call" | custom-call | tf_op jit(solution)/shard_map/pick/pallas_call | solution.py:195
  6.4 18.3 %all_to_all.15 = f32[16,65,1,128]{3,2,1,0:T(1,128)S(1)} all-to-all(f32[16,65,1,128]{3,2,1,0:T(1,128)S(1)} %bitcast.15), channel_id=1, replica_groups=mesh['grp'=16,'z'=8,'core'=2] {'grp'}, dimensions={0} | all-to-all | bytes 1064960 | tf_op jit(solution)/shard_map/all_to_all | solution.py:220
  24.8 0.4 add.1
  25.1 1.9 %collective-permute-start = (f32[8,24,128]{2,1,0:T(8,128)S(1)}, f32[8,24,128]{2,1,0:T(8,128)S(1)}, u32[]{:S(2)}, u32[]{:S(2)}) collective-permute-start(f32[8,24,128]{2,1,0:T(8,128)S(1)} %get-tuple-element.9), channel_id=1, source_target_pairs={{0,1},{1,0},{2,3},{3,2},{4,5},{5,4},{6,7},{7,6},{8,9},{9,8},{10,11... | collective-permute-start | bytes 294920 | tf_op jit(solution)/shard_map/ppermute | solution.py:233
  27.1 1.7 %store.1.stored = f32[8,96,8,128]{3,2,1,0:T(8,128)} custom-call(f32[8,96,8,128]{3,2,1,0:T(8,128)S(1)} %get-tuple-element.6.kept), custom_call_target="tpu_custom_call" | custom-call | tf_op jit(solution)/shard_map/store/pallas_call | solution.py:234
  28.8 0.0 copy-start
  28.8 0.0 collective-permute-done.other
  28.8 15.9 %all_to_all.16.parts = f32[8,24,128]{2,1,0:T(8,128)S(1)} all-to-all(f32[8,24,128]{2,1,0:T(8,128)S(1)} %join.1), channel_id=1, replica_groups=mesh['grp'=16,'z'=8,'core'=2] {'z'}, dimensions={0} | all-to-all | bytes 196608 | tf_op jit(solution)/shard_map/all_to_all | solution.py:251
  44.7 0.0 copy-done
  44.8 9.9 %all_to_all.17 = f32[16,24,128]{2,1,0:T(8,128)S(1)} all-to-all(f32[16,24,128]{2,1,0:T(8,128)S(1)} %final.1), channel_id=1, replica_groups=mesh['grp'=16,'z'=8,'core'=2] {'grp'}, dimensions={0} | all-to-all | bytes 393216 | tf_op jit(solution)/shard_map/all_to_all | solution.py:261
  54.6 0.7 %copy.11 = f32[64,768]{1,0:T(8,128)} copy(f32[64,768]{1,0:T(8,128)S(1)} %bitcast.18) | data formatting | bytes 393216
  (2 shorter events, 0.0 us)
Async XLA Ops:
  25.1 3.7 %collective-permute-start = (f32[8,24,128]{2,1,0:T(8,128)S(1)}, f32[8,24,128]{2,1,0:T(8,128)S(1)}, u32[]{:S(2)}, u32[]{:S(2)}) collective-permute-start(f32[8,24,128]{2,1,0:T(8,128)S(1)} %get-tuple-element.9), channel_id=1, source_target_pairs={{0,1},{1,0},{2,3},{3,2},{4,5},{5,4},{6,7},{7,6},{8,9},{9,8},{10,11... | collective-permute-start | bytes 294920 | tf_op jit(solution)/shard_map/ppermute | solution.py:233
  28.8 15.9 %copy-start = (f32[64,768]{1,0:T(8,128)S(1)}, f32[64,768]{1,0:T(8,128)}, u32[]{:S(2)}) copy-start(f32[64,768]{1,0:T(8,128)} %momentum.1) | copy-start | bytes 589828

commit v4 on v2

--- a/solution.py
+++ b/solution.py
@@ -3,6 +3,7 @@
 from jax import lax
 from jax.experimental import pallas as pl
 from jax.experimental.pallas import tpu as pltpu
+from jax.sharding import Mesh
 from jax.sharding import PartitionSpec as P
 
 momentum_decay = 0.9
@@ -16,7 +17,8 @@
                 small_sems, acts_sems, tile_sem, *, row_blocks, own_blocks):
     row_tiles = grad_ref.shape[0]
     slots = index.shape[1]
-    members = out_ref.shape[0]
+    rows = slots + 1
+    members = out_ref.shape[0] // rows
     half = own_blocks // 2
     part = half * sublanes
     chunk_blocks = row_blocks // chunk_count
@@ -70,7 +72,7 @@
     codes_v[0:1, 0:slots] = code
     both = codes_v[...]
     both = both + pltpu.roll(both, slots, 1)
-    out_ref[0, slots:slots + sublanes, :] = both
+    out_ref[slots:rows, :] = both[0:1]
 
     left.wait()
     for i in range(chunk_count):
@@ -96,18 +98,18 @@
         grad = grad_ref[high, col]
         grad_ref[high, col] = jnp.where(mine, -held, grad)
         tiles[s] = jnp.where(mine, held + grad, 0.0)
-        out_ref[0, pl.ds(s, 1), :] = tiles[s, pl.ds(low, 1), :]
+        out_ref[pl.ds(s, 1), :] = tiles[s, pl.ds(low, 1), :]
         return carry
 
     lax.fori_loop(0, slots, pick, 0, unroll=8)
-    message = out_ref[0]
+    message = out_ref[0:rows, :]
     for j in range(1, members):
-        out_ref[j] = message
-
-
-def add_kernel(held, out_ref, *, slots):
-    sources = held.shape[0]
-    rows = out_ref.shape[0]
+        out_ref[j * rows:(j + 1) * rows, :] = message
+
+
+def add_kernel(held, own_ref, other_ref, *, slots, rows):
+    step = slots + 1
+    sources = held.shape[0] // step
     base = lax.axis_index("grp") * rows
     target = (lax.broadcasted_iota(jnp.int32, (rows, lanes), 0) + base).astype(jnp.float32)
     low = lax.broadcasted_iota(jnp.int32, (1, lanes), 1) < slots
@@ -115,9 +117,13 @@
     for q in range(0, sources, 4):
         hits = []
         for p in (q, q + 2):
-            code = jnp.where(low, held[p, slots:slots + 1, :], held[p + 1, slots:slots + 1, :])
+            code = jnp.where(
+                low,
+                held[p * step + slots:(p + 1) * step, :],
+                held[(p + 1) * step + slots:(p + 2) * step, :],
+            )
             hits.append(jnp.where(target == code, 1.0, 0.0).astype(jnp.bfloat16))
-        values = jnp.concatenate([held[p, 0:slots, :] for p in range(q, q + 4)], axis=0)
+        values = jnp.concatenate([held[p * step:p * step + slots, :] for p in range(q, q + 4)], axis=0)
         high = values.astype(jnp.bfloat16)
         rest = (values - high.astype(jnp.float32)).astype(jnp.bfloat16)
         total = total + jnp.dot(
@@ -125,7 +131,18 @@
             jnp.concatenate([high, rest], axis=1),
             preferred_element_type=jnp.float32,
         )
-    out_ref[...] = total[:, :lanes] + total[:, lanes:]
+    total = total[:, :lanes] + total[:, lanes:]
+    part = rows // (2 * own_ref.shape[0])
+    second = lax.axis_index("core") == 1
+    for z in range(own_ref.shape[0]):
+        even = total[2 * z * part:(2 * z + 1) * part]
+        odd = total[(2 * z + 1) * part:(2 * z + 2) * part]
+        own_ref[z] = jnp.where(second, odd, even)
+        other_ref[z] = jnp.where(second, even, odd)
+
+
+def join_kernel(own, other, out_ref):
+    out_ref[...] = own[...] + other[...]
 
 
 def final_kernel(parts, momentum, out_ref):
@@ -133,7 +150,7 @@
     wide = part // sublanes * lanes
     me = lax.axis_index("grp")
     total = parts[0]
-    for j in range(1, members):
+    for j in range(1, parts.shape[0]):
         total = total + parts[j]
     rows = pl.ds(pl.multiple_of((me // 2) * sublanes, sublanes), sublanes)
     old = momentum[rows, pl.ds(pl.multiple_of((me % 2) * wide, lanes), wide)]
@@ -180,7 +197,7 @@
     row_blocks = width // lanes
     own_blocks = momentum_in.shape[1] // lanes
     members = lax.axis_size("grp")
-    owners = lax.axis_size("dev")
+    owners = lax.axis_size("z") * lax.axis_size("core")
     part = own_blocks // 2 * sublanes
     smem = pl.BlockSpec(memory_space=pltpu.SMEM)
     vmem = pl.BlockSpec(memory_space=pltpu.VMEM)
@@ -197,7 +214,7 @@
         out_specs=[vmem, vmem],
         out_shape=[
             pltpu.VMEM(tiled.shape, jnp.float32),
-            pltpu.VMEM((members, slots + sublanes, lanes), jnp.float32),
+            pltpu.VMEM((members * (slots + 1), lanes), jnp.float32),
         ],
         scratch_shapes=[
             pltpu.SMEM((1, slots), jnp.int32),
@@ -216,17 +233,29 @@
         in_hbm(sel_index), sel_count, in_hbm(grads_out.T), in_hbm(acts), in_hbm(tiled),
     )
 
-    held = lax.all_to_all(message, "grp", 0, 0, tiled=True)
-
-    sums = pl.pallas_call(
-        lambda *refs: add_kernel(*refs, slots=slots),
+    held = lax.all_to_all(
+        message.reshape(members, slots + 1, 1, lanes), "grp", 0, 0, tiled=True
+    ).reshape(message.shape)
+
+    shape = (lax.axis_size("z"), part, lanes)
+    own, other = pl.pallas_call(
+        lambda *refs: add_kernel(*refs, slots=slots, rows=owners * part),
         in_specs=[vmem],
-        out_specs=vmem,
-        out_shape=pltpu.VMEM((owners * part, lanes), jnp.float32),
+        out_specs=[vmem, vmem],
+        out_shape=[pltpu.VMEM(shape, jnp.float32), pltpu.VMEM(shape, jnp.float32)],
         compiler_params=pltpu.CompilerParams(vmem_limit_bytes=8 << 20),
         name="add",
     )(held)
-    parts = lax.all_to_all(sums.reshape(owners, part, lanes), "dev", 0, 0, tiled=True)
+    other = lax.ppermute(other, "core", [(0, 1), (1, 0)])
+    sums = pl.pallas_call(
+        join_kernel,
+        in_specs=[vmem, vmem],
+        out_specs=vmem,
+        out_shape=pltpu.VMEM(shape, jnp.float32),
+        compiler_params=pltpu.CompilerParams(vmem_limit_bytes=8 << 20),
+        name="join",
+    )(own, other)
+    parts = lax.all_to_all(sums, "z", 0, 0, tiled=True)
 
     new = pl.pallas_call(
         final_kernel,
@@ -257,18 +286,22 @@
 
 
 def solution(mesh):
+    groups, devices = mesh.devices.shape
+    split = Mesh(mesh.devices.reshape(groups, devices // 2, 2), ("grp", "z", "core"))
+    every = ("grp", "z", "core")
+    owner = ("z", "core")
     placed = (
-        P(("grp", "dev"), None),
-        P(("grp", "dev"), None),
-        P(("grp", "dev"), None, None),
-        P(("grp", "dev"), None),
-        P(("grp", "dev")),
-        P(None, "dev"),
+        P(every, None),
+        P(every, None),
+        P(every, None, None),
+        P(every, None),
+        P(every),
+        P(None, owner),
     )
     return jax.shard_map(
         local,
-        mesh=mesh,
+        mesh=split,
         in_specs=placed,
-        out_specs=(P(("grp", "dev"), None, None), P(None, "dev")),
+        out_specs=(P(every, None, None), P(None, owner)),
         check_vma=False,
     )

time: 57.9 us -> 55.6 us (0.960)
  blocking collectives: 39 us -> 33.7 us
  starting transfers between devices: 3.52 us -> 5.47 us
    all_to_all x2, blocking collectives: 39 us -> 33.7 us  [the longest x1 18.3 us: local(): lax.all_to_all(message.reshape(members, slots + 1, 1, lanes), 'grp', 0, 0...]
    ppermute x0 -> x1, starting transfers between devices: none -> 1.94 us  [local(): other = lax.ppermute(other, 'core', [(0, 1), (1, 0)])]
    ppermute x0 -> x1, waiting for transfers between devices: none -> 0.94 us  [local(): other = lax.ppermute(other, 'core', [(0, 1), (1, 0)])]
  transfers between devices with their start and end apart: 1 -> 2, of which waited for: 1 -> 2; matrix products, arithmetic and copies ran while one was open for 0% -> 0% of each run, Pallas kernels for 5% -> 5%
where the time goes in v4:
time: 55.6 us; the launch traced here: 54.8 us
  blocking collectives  33.7 us (61%)
  Pallas kernels  8.51 us (15%)
  starting transfers between devices  5.47 us (10%)
  waiting for transfers between devices  5.12 us (9%)
  between operations  1.32 us (2%)
  local copies, waits for them, and re-layouts  0.68 us (1%)
    all_to_all x1, blocking collectives, local(): lax.all_to_all(message.reshape(members, slots + 1, 1, lanes), 'grp', 0, 0...  18.3 us
    all_to_all x1, blocking collectives, local(): parts = lax.all_to_all(sums, 'z', 0, 0, tiled=True)  15.4 us
    pallas_call x1, Pallas kernels, local(): pl.pallas_call(pick, in_specs=[hbm, smem, hbm, hbm, hbm], out_specs=[vmem...  4.58 us
    all_to_all x1, waiting for transfers between devices, local(): whole = lax.all_to_all(new, 'grp', 0, 0, tiled=True)  4.17 us
    all_to_all x1, starting transfers between devices, local(): whole = lax.all_to_all(new, 'grp', 0, 0, tiled=True)  3.52 us
    pallas_call x1, Pallas kernels, local(): pl.pallas_call(keep_kernel, in_specs=[vmem, hbm], out_specs=hbm, out_shap...  2.84 us
    ppermute x1, starting transfers between devices, local(): other = lax.ppermute(other, 'core', [(0, 1), (1, 0)])  1.94 us
  transfers between devices with their start and end apart: 2, of which 2 were waited for; matrix products, arithmetic and copies ran while one was open for 0% of the time, Pallas kernels for 5%

profile of v4, /device:TPU:1, one launch (start us, length us, event | category | flops | bytes accessed | tf_op | source)
XLA Modules:
  0.0 54.8 jit_solution(17614739662303448204)
XLA Ops:
  1.3 0.0 copy-start
  1.3 4.6 %pick.1 = (f32[8,96,8,128]{3,2,1,0:T(8,128)S(1)}, f32[1040,128]{1,0:T(8,128)S(1)}) custom-call(s32[1,64]{1,0:T(1,128)} %refs_0_.1, s32[1]{0:T(128)S(6)} %copy.10.refs_1_, bf16[64,256]{1,0:T(8,128)(2,1)} %bitcast.20, bf16[256,12288]{1,0:T(8,128)(2,1)} %refs_3_.1, f32[8,96,8,128]{3,2,1,0:T(8,128)} %bitcast.16), custom_call_target="tpu_custom_call" | custom-call | tf_op jit(solution)/shard_map/pick/pallas_call | solution.py:211
  5.9 18.3 %all_to_all.15 = f32[16,65,1,128]{3,2,1,0:T(1,128)S(1)} all-to-all(f32[16,65,1,128]{3,2,1,0:T(1,128)S(1)} %bitcast.15), channel_id=1, replica_groups=mesh['grp'=16,'z'=8,'core'=2] {'grp'}, dimensions={0} | all-to-all | bytes 1064960 | tf_op jit(solution)/shard_map/all_to_all | solution.py:236
  24.2 0.4 add.1
  24.6 1.9 %collective-permute-start = (f32[8,24,128]{2,1,0:T(8,128)S(1)}, f32[8,24,128]{2,1,0:T(8,128)S(1)}, u32[]{:S(2)}, u32[]{:S(2)}) collective-permute-start(f32[8,24,128]{2,1,0:T(8,128)S(1)} %get-tuple-element.9), channel_id=1, source_target_pairs={{0,1},{1,0},{2,3},{3,2},{4,5},{5,4},{6,7},{7,6},{8,9},{9,8},{10,11... | collective-permute-start | bytes 294920 | tf_op jit(solution)/shard_map/ppermute | solution.py:249
  26.5 0.9 %collective-permute-done.other = f32[8,24,128]{2,1,0:T(8,128)S(1)} collective-permute-done((f32[8,24,128]{2,1,0:T(8,128)S(1)}, f32[8,24,128]{2,1,0:T(8,128)S(1)}, u32[]{:S(2)}, u32[]{:S(2)}) %collective-permute-start) | collective-permute-done | bytes 98336 | tf_op jit(solution)/shard_map/ppermute | solution.py:249
  27.5 15.4 %all_to_all.16.parts = f32[8,24,128]{2,1,0:T(8,128)S(1)} all-to-all(f32[8,24,128]{2,1,0:T(8,128)S(1)} %join.1), channel_id=1, replica_groups=mesh['grp'=16,'z'=8,'core'=2] {'z'}, dimensions={0} | all-to-all | bytes 196608 | tf_op jit(solution)/shard_map/all_to_all | solution.py:258
  42.9 0.0 copy-done
  42.9 0.7 %final.1 = f32[16,24,128]{2,1,0:T(8,128)} custom-call(f32[8,24,128]{2,1,0:T(8,128)S(1)} %all_to_all.16.parts, f32[64,768]{1,0:T(8,128)S(1)} %copy-done), custom_call_target="tpu_custom_call" | custom-call | tf_op jit(solution)/shard_map/final/pallas_call | solution.py:260
  43.6 3.5 %all-to-all-start.2 = ((f32[16,24,128]{2,1,0:T(8,128)}), f32[16,24,128]{2,1,0:T(8,128)S(1)}, u32[]{:S(2)}, u32[]{:S(2)}) async-start(f32[16,24,128]{2,1,0:T(8,128)} %final.1), calls=%async_computation.2 | async-start | bytes 393216 | tf_op jit(solution)/shard_map/all_to_all | solution.py:268
  47.1 2.8 %keep.1 = f32[8,96,8,128]{3,2,1,0:T(8,128)} custom-call(f32[8,96,8,128]{3,2,1,0:T(8,128)S(1)} %get-tuple-element.6.grad, f32[8,96,8,128]{3,2,1,0:T(8,128)} %bitcast.17), custom_call_target="tpu_custom_call" | custom-call | tf_op jit(solution)/shard_map/keep/pallas_call | solution.py:271
  50.0 4.2 %all-to-all-done.2 = f32[16,24,128]{2,1,0:T(8,128)S(1)} async-done(((f32[16,24,128]{2,1,0:T(8,128)}), f32[16,24,128]{2,1,0:T(8,128)S(1)}, u32[]{:S(2)}, u32[]{:S(2)}) %all-to-all-start.2) | async-done | bytes 196640 | tf_op jit(solution)/shard_map/all_to_all | solution.py:268
  54.2 0.7 %copy.11 = f32[64,768]{1,0:T(8,128)} copy(f32[64,768]{1,0:T(8,128)S(1)} %bitcast.19) | data formatting | bytes 393216
  (1 shorter events, 0.0 us)
Async XLA Ops:
  1.3 41.6 %copy-start = (f32[64,768]{1,0:T(8,128)S(1)}, f32[64,768]{1,0:T(8,128)}, u32[]{:S(2)}) copy-start(f32[64,768]{1,0:T(8,128)} %momentum.1) | copy-start | bytes 589828
  24.6 2.9 %collective-permute-start = (f32[8,24,128]{2,1,0:T(8,128)S(1)}, f32[8,24,128]{2,1,0:T(8,128)S(1)}, u32[]{:S(2)}, u32[]{:S(2)}) collective-permute-start(f32[8,24,128]{2,1,0:T(8,128)S(1)} %get-tuple-element.9), channel_id=1, source_target_pairs={{0,1},{1,0},{2,3},{3,2},{4,5},{5,4},{6,7},{7,6},{8,9},{9,8},{10,11... | collective-permute-start | bytes 294920 | tf_op jit(solution)/shard_map/ppermute | solution.py:249
  43.6 10.6 %all-to-all-start.2 = ((f32[16,24,128]{2,1,0:T(8,128)}), f32[16,24,128]{2,1,0:T(8,128)S(1)}, u32[]{:S(2)}, u32[]{:S(2)}) async-start(f32[16,24,128]{2,1,0:T(8,128)} %final.1), calls=%async_computation.2 | async-start | bytes 393216 | tf_op jit(solution)/shard_map/all_to_all | solution.py:268

commit v5 on v4

--- a/solution.py
+++ b/solution.py
@@ -145,7 +145,7 @@
     out_ref[...] = own[...] + other[...]
 
 
-def final_kernel(parts, momentum, out_ref):
+def final_kernel(parts, momentum, kept, out_ref):
     members, part, _ = out_ref.shape
     wide = part // sublanes * lanes
     me = lax.axis_index("grp")
@@ -257,17 +257,6 @@
     )(own, other)
     parts = lax.all_to_all(sums, "z", 0, 0, tiled=True)
 
-    new = pl.pallas_call(
-        final_kernel,
-        in_specs=[vmem, vmem],
-        out_specs=vmem,
-        out_shape=pltpu.VMEM((members, part, lanes), jnp.float32),
-        compiler_params=pltpu.CompilerParams(vmem_limit_bytes=8 << 20),
-        name="final",
-    )(parts, momentum_in)
-    whole = lax.all_to_all(new, "grp", 0, 0, tiled=True)
-    whole = whole.reshape(columns // sublanes, 2, own_blocks // 2, sublanes, lanes)
-    whole = whole.transpose(0, 3, 1, 2, 4).reshape(columns, own_blocks * lanes)
     kept = pl.pallas_call(
         keep_kernel,
         in_specs=[vmem, hbm],
@@ -281,6 +270,17 @@
         compiler_params=pltpu.CompilerParams(vmem_limit_bytes=8 << 20),
         name="keep",
     )(pltpu.with_memory_space_constraint(grad, pltpu.VMEM), in_hbm(tiled))
+    new = pl.pallas_call(
+        final_kernel,
+        in_specs=[vmem, vmem, hbm],
+        out_specs=vmem,
+        out_shape=pltpu.VMEM((members, part, lanes), jnp.float32),
+        compiler_params=pltpu.CompilerParams(vmem_limit_bytes=8 << 20),
+        name="final",
+    )(parts, momentum_in, in_hbm(kept))
+    whole = lax.all_to_all(new, "grp", 0, 0, tiled=True)
+    whole = whole.reshape(columns // sublanes, 2, own_blocks // 2, sublanes, lanes)
+    whole = whole.transpose(0, 3, 1, 2, 4).reshape(columns, own_blocks * lanes)
     kept = kept.transpose(0, 2, 1, 3).reshape(residual_in.shape)
     return (kept, whole)
 

time: 55.6 us -> 55.3 us (level)
  blocking collectives: 33.7 us -> 28.3 us
  starting transfers between devices: 5.47 us -> 10.1 us
    all_to_all x1, blocking collectives: 15.4 us -> 9.97 us  [local(): whole = lax.all_to_all(new, 'grp', 0, 0, tiled=True)]
    all_to_all x1, starting transfers between devices: 3.52 us -> 8.18 us  [local(): parts = lax.all_to_all(sums, 'z', 0, 0, tiled=True)]
    pallas_call x1, Pallas kernels: 0.7 us -> 0.03 us  [local(): pl.pallas_call(final_kernel, in_specs=[vmem, vmem, hbm], out_specs=vmem,...]
    pallas_call x1, Pallas kernels: 0.01 us -> 0.65 us  [local(): pl.pallas_call(join_kernel, in_specs=[vmem, vmem], out_specs=vmem, out_sh...]
where the time goes in v5:
time: 55.3 us; the launch traced here: 54.4 us
  blocking collectives  28.3 us (51%)
  starting transfers between devices  10.1 us (18%)
  Pallas kernels  8.47 us (15%)
  waiting for transfers between devices  5.5 us (10%)
  between operations  1.31 us (2%)
  local copies, waits for them, and re-layouts  0.68 us (1%)
    all_to_all x1, blocking collectives, local(): lax.all_to_all(message.reshape(members, slots + 1, 1, lanes), 'grp', 0, 0...  18.3 us
    all_to_all x1, blocking collectives, local(): whole = lax.all_to_all(new, 'grp', 0, 0, tiled=True)  9.97 us
    all_to_all x1, starting transfers between devices, local(): parts = lax.all_to_all(sums, 'z', 0, 0, tiled=True)  8.18 us
    all_to_all x1, waiting for transfers between devices, local(): parts = lax.all_to_all(sums, 'z', 0, 0, tiled=True)  4.56 us
    pallas_call x1, Pallas kernels, local(): pl.pallas_call(pick, in_specs=[hbm, smem, hbm, hbm, hbm], out_specs=[vmem...  4.54 us
    pallas_call x1, Pallas kernels, local(): pl.pallas_call(keep_kernel, in_specs=[vmem, hbm], out_specs=hbm, out_shap...  2.88 us
    ppermute x1, starting transfers between devices, local(): other = lax.ppermute(other, 'core', [(0, 1), (1, 0)])  1.94 us
  transfers between devices with their start and end apart: 2, of which 2 were waited for; matrix products, arithmetic and copies ran while one was open for 0% of the time, Pallas kernels for 5%

profile of v5, /device:TPU:1, one launch (start us, length us, event | category | flops | bytes accessed | tf_op | source)
XLA Modules:
  0.0 54.4 jit_solution(15772601723809258164)
XLA Ops:
  1.3 4.5 %pick.1 = (f32[8,96,8,128]{3,2,1,0:T(8,128)S(1)}, f32[1040,128]{1,0:T(8,128)S(1)}) custom-call(s32[1,64]{1,0:T(1,128)} %refs_0_.1, s32[1]{0:T(128)S(6)} %copy.10.refs_1_, bf16[64,256]{1,0:T(8,128)(2,1)} %bitcast.20, bf16[256,12288]{1,0:T(8,128)(2,1)} %refs_3_.1, f32[8,96,8,128]{3,2,1,0:T(8,128)} %bitcast.16), custom_call_target="tpu_custom_call" | custom-call | tf_op jit(solution)/shard_map/pick/pallas_call | solution.py:211
  5.8 18.3 %all_to_all.15 = f32[16,65,1,128]{3,2,1,0:T(1,128)S(1)} all-to-all(f32[16,65,1,128]{3,2,1,0:T(1,128)S(1)} %bitcast.15), channel_id=1, replica_groups=mesh['grp'=16,'z'=8,'core'=2] {'grp'}, dimensions={0} | all-to-all | bytes 1064960 | tf_op jit(solution)/shard_map/all_to_all | solution.py:236
  24.1 0.4 add.1
  24.5 1.9 %collective-permute-start = (f32[8,24,128]{2,1,0:T(8,128)S(1)}, f32[8,24,128]{2,1,0:T(8,128)S(1)}, u32[]{:S(2)}, u32[]{:S(2)}) collective-permute-start(f32[8,24,128]{2,1,0:T(8,128)S(1)} %get-tuple-element.9), channel_id=1, source_target_pairs={{0,1},{1,0},{2,3},{3,2},{4,5},{5,4},{6,7},{7,6},{8,9},{9,8},{10,11... | collective-permute-start | bytes 294920 | tf_op jit(solution)/shard_map/ppermute | solution.py:249
  26.5 0.9 %collective-permute-done.other = f32[8,24,128]{2,1,0:T(8,128)S(1)} collective-permute-done((f32[8,24,128]{2,1,0:T(8,128)S(1)}, f32[8,24,128]{2,1,0:T(8,128)S(1)}, u32[]{:S(2)}, u32[]{:S(2)}) %collective-permute-start) | collective-permute-done | bytes 98336 | tf_op jit(solution)/shard_map/ppermute | solution.py:249
  27.4 0.7 %join.1 = f32[8,24,128]{2,1,0:T(8,128)} custom-call(f32[8,24,128]{2,1,0:T(8,128)S(1)} %get-tuple-element.8.own, f32[8,24,128]{2,1,0:T(8,128)S(1)} %collective-permute-done.other), custom_call_target="tpu_custom_call" | custom-call | tf_op jit(solution)/shard_map/join/pallas_call | solution.py:250
  28.1 8.2 %all-to-all-start.1 = ((f32[8,24,128]{2,1,0:T(8,128)}), f32[8,24,128]{2,1,0:T(8,128)S(1)}, u32[]{:S(2)}, u32[]{:S(2)}) async-start(f32[8,24,128]{2,1,0:T(8,128)} %join.1), calls=%async_computation.1 | async-start | bytes 196608 | tf_op jit(solution)/shard_map/all_to_all | solution.py:258
  36.2 0.0 copy-start
  36.2 2.9 %keep.1.kept = f32[8,96,8,128]{3,2,1,0:T(8,128)} custom-call(f32[8,96,8,128]{3,2,1,0:T(8,128)S(1)} %get-tuple-element.6.grad, f32[8,96,8,128]{3,2,1,0:T(8,128)} %bitcast.17), custom_call_target="tpu_custom_call" | custom-call | tf_op jit(solution)/shard_map/keep/pallas_call | solution.py:260
  39.1 4.6 %all-to-all-done.1.parts = f32[8,24,128]{2,1,0:T(8,128)S(1)} async-done(((f32[8,24,128]{2,1,0:T(8,128)}), f32[8,24,128]{2,1,0:T(8,128)S(1)}, u32[]{:S(2)}, u32[]{:S(2)}) %all-to-all-start.1) | async-done | bytes 98336 | tf_op jit(solution)/shard_map/all_to_all | solution.py:258
  43.7 0.0 copy-done
  43.7 10.0 %all_to_all.16 = f32[16,24,128]{2,1,0:T(8,128)S(1)} all-to-all(f32[16,24,128]{2,1,0:T(8,128)S(1)} %final.1), channel_id=1, replica_groups=mesh['grp'=16,'z'=8,'core'=2] {'grp'}, dimensions={0} | all-to-all | bytes 393216 | tf_op jit(solution)/shard_map/all_to_all | solution.py:281
  53.7 0.7 %copy.11 = f32[64,768]{1,0:T(8,128)} copy(f32[64,768]{1,0:T(8,128)S(1)} %bitcast.19) | data formatting | bytes 393216
  (1 shorter events, 0.0 us)
Async XLA Ops:
  24.5 2.9 %collective-permute-start = (f32[8,24,128]{2,1,0:T(8,128)S(1)}, f32[8,24,128]{2,1,0:T(8,128)S(1)}, u32[]{:S(2)}, u32[]{:S(2)}) collective-permute-start(f32[8,24,128]{2,1,0:T(8,128)S(1)} %get-tuple-element.9), channel_id=1, source_target_pairs={{0,1},{1,0},{2,3},{3,2},{4,5},{5,4},{6,7},{7,6},{8,9},{9,8},{10,11... | collective-permute-start | bytes 294920 | tf_op jit(solution)/shard_map/ppermute | solution.py:249
  28.1 15.6 %all-to-all-start.1 = ((f32[8,24,128]{2,1,0:T(8,128)}), f32[8,24,128]{2,1,0:T(8,128)S(1)}, u32[]{:S(2)}, u32[]{:S(2)}) async-start(f32[8,24,128]{2,1,0:T(8,128)} %join.1), calls=%async_computation.1 | async-start | bytes 196608 | tf_op jit(solution)/shard_map/all_to_all | solution.py:258
  36.2 7.5 %copy-start = (f32[64,768]{1,0:T(8,128)S(1)}, f32[64,768]{1,0:T(8,128)}, u32[]{:S(2)}) copy-start(f32[64,768]{1,0:T(8,128)} %momentum.1) | copy-start | bytes 589828

commit v6 on v5

--- a/solution.py
+++ b/solution.py
@@ -9,7 +9,7 @@
 momentum_decay = 0.9
 lanes = 128
 sublanes = 8
-chunk_count = 3
+chunk_count = 2
 
 
 def pick_kernel(index, count_s, grads_t, acts, residual, grad_ref, out_ref,

time: 55.3 us -> 55.4 us (level)
  no operation moved by 1% of the time
where the time goes in v6:
time: 55.4 us; the launch traced here: 54.4 us
  blocking collectives  28.3 us (51%)
  starting transfers between devices  10.1 us (18%)
  Pallas kernels  8.53 us (15%)
  waiting for transfers between devices  5.5 us (10%)
  between operations  1.31 us (2%)
  local copies, waits for them, and re-layouts  0.68 us (1%)
    all_to_all x1, blocking collectives, local(): lax.all_to_all(message.reshape(members, slots + 1, 1, lanes), 'grp', 0, 0...  18.3 us
    all_to_all x1, blocking collectives, local(): whole = lax.all_to_all(new, 'grp', 0, 0, tiled=True)  9.97 us
    all_to_all x1, starting transfers between devices, local(): parts = lax.all_to_all(sums, 'z', 0, 0, tiled=True)  8.19 us
    pallas_call x1, Pallas kernels, local(): pl.pallas_call(pick, in_specs=[hbm, smem, hbm, hbm, hbm], out_specs=[vmem...  4.6 us
    all_to_all x1, waiting for transfers between devices, local(): parts = lax.all_to_all(sums, 'z', 0, 0, tiled=True)  4.56 us
    pallas_call x1, Pallas kernels, local(): pl.pallas_call(keep_kernel, in_specs=[vmem, hbm], out_specs=hbm, out_shap...  2.88 us
    ppermute x1, starting transfers between devices, local(): other = lax.ppermute(other, 'core', [(0, 1), (1, 0)])  1.94 us
  transfers between devices with their start and end apart: 2, of which 2 were waited for; matrix products, arithmetic and copies ran while one was open for 0% of the time, Pallas kernels for 5%

profile of v6, /device:TPU:1, one launch (start us, length us, event | category | flops | bytes accessed | tf_op | source)
XLA Modules:
  0.0 54.4 jit_solution(14546103052529797245)
XLA Ops:
  1.3 4.6 %pick.1 = (f32[8,96,8,128]{3,2,1,0:T(8,128)S(1)}, f32[1040,128]{1,0:T(8,128)S(1)}) custom-call(s32[1,64]{1,0:T(1,128)} %refs_0_.1, s32[1]{0:T(128)S(6)} %copy.10.refs_1_, bf16[64,256]{1,0:T(8,128)(2,1)} %bitcast.20, bf16[256,12288]{1,0:T(8,128)(2,1)} %refs_3_.1, f32[8,96,8,128]{3,2,1,0:T(8,128)} %bitcast.16), custom_call_target="tpu_custom_call" | custom-call | tf_op jit(solution)/shard_map/pick/pallas_call | solution.py:211
  5.9 18.3 %all_to_all.15 = f32[16,65,1,128]{3,2,1,0:T(1,128)S(1)} all-to-all(f32[16,65,1,128]{3,2,1,0:T(1,128)S(1)} %bitcast.15), channel_id=1, replica_groups=mesh['grp'=16,'z'=8,'core'=2] {'grp'}, dimensions={0} | all-to-all | bytes 1064960 | tf_op jit(solution)/shard_map/all_to_all | solution.py:236
  24.2 0.4 add.1
  24.6 1.9 %collective-permute-start = (f32[8,24,128]{2,1,0:T(8,128)S(1)}, f32[8,24,128]{2,1,0:T(8,128)S(1)}, u32[]{:S(2)}, u32[]{:S(2)}) collective-permute-start(f32[8,24,128]{2,1,0:T(8,128)S(1)} %get-tuple-element.9), channel_id=1, source_target_pairs={{0,1},{1,0},{2,3},{3,2},{4,5},{5,4},{6,7},{7,6},{8,9},{9,8},{10,11... | collective-permute-start | bytes 294920 | tf_op jit(solution)/shard_map/ppermute | solution.py:249
  26.5 0.9 %collective-permute-done.other = f32[8,24,128]{2,1,0:T(8,128)S(1)} collective-permute-done((f32[8,24,128]{2,1,0:T(8,128)S(1)}, f32[8,24,128]{2,1,0:T(8,128)S(1)}, u32[]{:S(2)}, u32[]{:S(2)}) %collective-permute-start) | collective-permute-done | bytes 98336 | tf_op jit(solution)/shard_map/ppermute | solution.py:249
  27.5 0.7 %join.1 = f32[8,24,128]{2,1,0:T(8,128)} custom-call(f32[8,24,128]{2,1,0:T(8,128)S(1)} %get-tuple-element.8.own, f32[8,24,128]{2,1,0:T(8,128)S(1)} %collective-permute-done.other), custom_call_target="tpu_custom_call" | custom-call | tf_op jit(solution)/shard_map/join/pallas_call | solution.py:250
  28.1 8.2 %all-to-all-start.1 = ((f32[8,24,128]{2,1,0:T(8,128)}), f32[8,24,128]{2,1,0:T(8,128)S(1)}, u32[]{:S(2)}, u32[]{:S(2)}) async-start(f32[8,24,128]{2,1,0:T(8,128)} %join.1), calls=%async_computation.1 | async-start | bytes 196608 | tf_op jit(solution)/shard_map/all_to_all | solution.py:258
  36.3 0.0 copy-start
  36.3 2.9 %keep.1.kept = f32[8,96,8,128]{3,2,1,0:T(8,128)} custom-call(f32[8,96,8,128]{3,2,1,0:T(8,128)S(1)} %get-tuple-element.6.grad, f32[8,96,8,128]{3,2,1,0:T(8,128)} %bitcast.17), custom_call_target="tpu_custom_call" | custom-call | tf_op jit(solution)/shard_map/keep/pallas_call | solution.py:260
  39.2 4.6 %all-to-all-done.1.parts = f32[8,24,128]{2,1,0:T(8,128)S(1)} async-done(((f32[8,24,128]{2,1,0:T(8,128)}), f32[8,24,128]{2,1,0:T(8,128)S(1)}, u32[]{:S(2)}, u32[]{:S(2)}) %all-to-all-start.1) | async-done | bytes 98336 | tf_op jit(solution)/shard_map/all_to_all | solution.py:258
  43.7 0.0 copy-done
  43.8 10.0 %all_to_all.16 = f32[16,24,128]{2,1,0:T(8,128)S(1)} all-to-all(f32[16,24,128]{2,1,0:T(8,128)S(1)} %final.1), channel_id=1, replica_groups=mesh['grp'=16,'z'=8,'core'=2] {'grp'}, dimensions={0} | all-to-all | bytes 393216 | tf_op jit(solution)/shard_map/all_to_all | solution.py:281
  53.8 0.7 %copy.11 = f32[64,768]{1,0:T(8,128)} copy(f32[64,768]{1,0:T(8,128)S(1)} %bitcast.19) | data formatting | bytes 393216
  (1 shorter events, 0.0 us)
Async XLA Ops:
  24.6 2.9 %collective-permute-start = (f32[8,24,128]{2,1,0:T(8,128)S(1)}, f32[8,24,128]{2,1,0:T(8,128)S(1)}, u32[]{:S(2)}, u32[]{:S(2)}) collective-permute-start(f32[8,24,128]{2,1,0:T(8,128)S(1)} %get-tuple-element.9), channel_id=1, source_target_pairs={{0,1},{1,0},{2,3},{3,2},{4,5},{5,4},{6,7},{7,6},{8,9},{9,8},{10,11... | collective-permute-start | bytes 294920 | tf_op jit(solution)/shard_map/ppermute | solution.py:249
  28.1 15.6 %all-to-all-start.1 = ((f32[8,24,128]{2,1,0:T(8,128)}), f32[8,24,128]{2,1,0:T(8,128)S(1)}, u32[]{:S(2)}, u32[]{:S(2)}) async-start(f32[8,24,128]{2,1,0:T(8,128)} %join.1), calls=%async_computation.1 | async-start | bytes 196608 | tf_op jit(solution)/shard_map/all_to_all | solution.py:258
  36.3 7.5 %copy-start = (f32[64,768]{1,0:T(8,128)S(1)}, f32[64,768]{1,0:T(8,128)}, u32[]{:S(2)}) copy-start(f32[64,768]{1,0:T(8,128)} %momentum.1) | copy-start | bytes 589828
